TPU v7x, 512 devices: a whole 4x8x8 slice. The times are simulated.
512 devices in a mesh: mem: 32 (over z_hi, y, core), kvh: 4 (over z_lo), row: 4 (over x).
Axes of the slice: x: 4, y: 8, z: 8 (z_hi: 2, z_lo: 4; z = z_hi * 4 + z_lo), core: 2. Of those that a mesh axis runs over, the one named last changes fastest.
Arguments:
- queries: bfloat16 [1024, 8192], P(('mem', 'kvh', 'row')), may hold values from -120 to 120
- output_gradient: bfloat16 [1024, 8192], P(('mem', 'kvh', 'row')), may hold values from -6 to 6
- keys: bfloat16 [24576, 1024], P('mem', 'kvh'), may hold values from -6 to 6
- values: bfloat16 [24576, 1024], P('mem', 'kvh'), may hold values from -6 to 6
- text_video: int32 [128, 8], P(None, 'row'), may hold values from 0 to 95
- video_blocks: int32 [96], replicated, may hold values from 1 to 4, 192 in all
Outputs:
- attention_out: bfloat16 [1024, 8192], P(('mem', 'kvh', 'row'))
- query_grad: bfloat16 [1024, 8192], P(('mem', 'kvh', 'row'))
- keys_gradient: bfloat16 [24576, 1024], P('mem', 'kvh')
- values_gradient: bfloat16 [24576, 1024], P('mem', 'kvh')
Inputs may be any that keep to these rules, and one draw needn't show every extreme that they name: Row sees images 0 to text_video. `video_blocks`: they sum to 192.
All inputs are finite; a program needn't handle non-finite values.
Results may differ from a plain program's by a relative error of at most 0.015.
Values may be sent and summed in bfloat16 or wider, within the bound.
A program may use at most 64 MiB of HBM per device.

v0:
```python
import jax
import jax.numpy as jnp
from jax import lax
from jax.sharding import PartitionSpec as P

QUERY_HEADS = 64
KEY_VALUE_HEADS = 8
HEAD_WIDTH = 128
FRAME = 128


masked_score = -1e30


def in_one_piece(arrays, axis, dim, along):
    both = jnp.concatenate(arrays, axis=along)
    result, at, outs = (lax.all_gather(both, axis, axis=dim, tiled=True), 0, [])
    for a in arrays:
        outs.append(lax.slice_in_dim(result, at, at + a.shape[along], axis=along))
        at += a.shape[along]
    return tuple(outs)


def sent_to_all(array, axis):
    count = lax.axis_size(axis)
    return lax.all_to_all(
        jnp.broadcast_to(array[None], (count, *array.shape)), axis, 0, 0, tiled=True
    )


def of_everyone(array, axis):
    everything = sent_to_all(array, axis)
    return jnp.sum(everything.astype(jnp.float32), axis=0)


def cut_along(array, dim, count):
    before, after = (array.shape[:dim], array.shape[dim + 1 :])
    return jnp.moveaxis(array.reshape(*before, count, -1, *after), dim, 0)


def sent_and_summed(array, axis, dim):
    pieces = cut_along(array, dim, lax.axis_size(axis))
    arrived = lax.all_to_all(pieces, axis, split_axis=0, concat_axis=0, tiled=True)
    return arrived.astype(jnp.float32).sum(axis=0)


def video_of_block(video_blocks, first_block, block_count):
    block_ends = jnp.cumsum(video_blocks)
    blocks = first_block + jnp.arange(block_count, dtype=jnp.int32)
    return jnp.sum((block_ends[None, :] <= blocks[:, None]).astype(jnp.int32), axis=1)


def per_device(queries, output_gradient, keys, values, text_video, video_blocks):
    inverse_root = HEAD_WIDTH ** (-0.5)
    heads_per_group = QUERY_HEADS // KEY_VALUE_HEADS
    mem_count = lax.axis_size("mem")
    local_query, local_grad = (
        lax.all_to_all(queries, "kvh", split_axis=1, concat_axis=0, tiled=True),
        lax.all_to_all(output_gradient, "kvh", split_axis=1, concat_axis=0, tiled=True),
    )
    query_rows, grad_rows = in_one_piece((local_query, local_grad), "mem", 0, 1)
    group_size = query_rows.shape[0]
    own_count = local_query.shape[0]
    key_local = keys.shape[1] // HEAD_WIDTH
    frames = keys.shape[0] // FRAME
    query_four = query_rows.reshape(group_size, key_local, heads_per_group, HEAD_WIDTH)
    grad_four = grad_rows.reshape(group_size, key_local, heads_per_group, HEAD_WIDTH)
    key_frames = keys.reshape(frames, FRAME, key_local, HEAD_WIDTH)
    value_frames = values.reshape(frames, FRAME, key_local, HEAD_WIDTH)
    key_video = video_of_block(video_blocks, lax.axis_index("mem") * frames, frames)
    visible = key_video[None, :] <= text_video.reshape(group_size)[:, None]
    frame_ids = jnp.arange(frames, dtype=jnp.int32)

    def frame_scores(frame_index):
        key_block = lax.dynamic_index_in_dim(key_frames, frame_index, 0, keepdims=False)
        scores = (
            jnp.einsum("rghd,jgd->rghj", query_four, key_block, preferred_element_type=jnp.float32)
            * inverse_root
        )
        seen_rows = lax.dynamic_index_in_dim(visible, frame_index, 1, keepdims=False)[
            :, None, None, None
        ]
        return (jnp.where(seen_rows, scores, masked_score), seen_rows, key_block)

    def forward_step(running, frame_index):
        running_top, totals, numerator = running
        scores, seen_rows, key_block = frame_scores(frame_index)
        new_top = jnp.maximum(running_top, jnp.max(scores, axis=3))
        weight = jnp.where(seen_rows, jnp.exp(scores - new_top[..., None]), 0.0)
        shrink_factor = jnp.exp(running_top - new_top)
        totals = totals * shrink_factor + jnp.sum(weight, axis=3)
        value_block = lax.dynamic_index_in_dim(value_frames, frame_index, 0, keepdims=False)
        numerator = numerator * shrink_factor[..., None] + jnp.einsum(
            "rghj,jgd->rghd",
            weight.astype(jnp.bfloat16),
            value_block,
            preferred_element_type=jnp.float32,
        )
        return ((new_top, totals, numerator), None)

    stat_shape = (group_size, key_local, heads_per_group)
    start_state = (
        jnp.full(stat_shape, masked_score, jnp.float32),
        jnp.zeros(stat_shape, jnp.float32),
        jnp.zeros(stat_shape + (HEAD_WIDTH,), jnp.float32),
    )
    (local_top, local_totals, numerator), unused = lax.scan(forward_step, start_state, frame_ids)
    own_grad = local_grad.reshape(own_count, key_local, heads_per_group, HEAD_WIDTH).astype(
        jnp.float32
    )
    sent = (
        numerator.reshape((mem_count, own_count) + numerator.shape[1:]),
        local_top.reshape((mem_count, own_count) + stat_shape[1:]),
        local_totals.reshape((mem_count, own_count) + stat_shape[1:]),
    )
    numerator_src, top_src, totals_src = (
        lax.all_to_all(sent[0], "mem", split_axis=0, concat_axis=0, tiled=True),
        lax.all_to_all(sent[1], "mem", split_axis=0, concat_axis=0, tiled=True),
        lax.all_to_all(sent[2], "mem", split_axis=0, concat_axis=0, tiled=True),
    )
    own_top = jnp.max(top_src, axis=0)
    factor = jnp.exp(top_src - own_top)
    own_totals = jnp.sum(totals_src * factor, axis=0)
    attention = jnp.sum(numerator_src * factor[..., None], axis=0) / own_totals[..., None]
    delta_own = jnp.sum(own_grad * attention, axis=3)
    own_log = own_top + jnp.log(own_totals)
    log_mass, delta_rows = in_one_piece((own_log, delta_own), "mem", 0, 1)
    attention_low = attention.reshape(own_count, key_local * heads_per_group * HEAD_WIDTH).astype(
        jnp.bfloat16
    )

    def backward_step(query_grad, frame_index):
        scores, seen_rows, key_block = frame_scores(frame_index)
        value_block = lax.dynamic_index_in_dim(value_frames, frame_index, 0, keepdims=False)
        probability = jnp.where(seen_rows, jnp.exp(scores - log_mass[..., None]), 0.0)
        prob_grad = jnp.einsum(
            "rghd,jgd->rghj", grad_four, value_block, preferred_element_type=jnp.float32
        )
        score_grad = (probability * (prob_grad - delta_rows[..., None])).astype(jnp.bfloat16)
        query_grad = (
            query_grad
            + jnp.einsum(
                "rghj,jgd->rghd", score_grad, key_block, preferred_element_type=jnp.float32
            )
            * inverse_root
        )
        key_part = (
            jnp.einsum("rghj,rghd->jgd", score_grad, query_four, preferred_element_type=jnp.float32)
            * inverse_root
        )
        value_part = jnp.einsum(
            "rghj,rghd->jgd",
            probability.astype(jnp.bfloat16),
            grad_four,
            preferred_element_type=jnp.float32,
        )
        return (query_grad, (key_part, value_part))

    query_grad, (key_parts, value_parts) = lax.scan(
        backward_step, jnp.zeros(stat_shape + (HEAD_WIDTH,), jnp.float32), frame_ids
    )
    key_sum = key_parts.reshape(keys.shape)
    value_sum = value_parts.reshape(values.shape)
    key_sum, value_sum = (
        of_everyone(key_sum.astype(jnp.bfloat16), "row").astype(jnp.float32),
        of_everyone(value_sum.astype(jnp.bfloat16), "row").astype(jnp.float32),
    )
    own_query_grad = sent_and_summed(query_grad.astype(jnp.bfloat16), "mem", 0)
    query_low = own_query_grad.reshape(own_count, key_local * heads_per_group * HEAD_WIDTH).astype(
        jnp.bfloat16
    )
    attention_text, query_text = (
        lax.all_to_all(attention_low, "kvh", split_axis=0, concat_axis=1, tiled=True),
        lax.all_to_all(query_low, "kvh", split_axis=0, concat_axis=1, tiled=True),
    )
    return (
        attention_text,
        query_text,
        key_sum.astype(jnp.bfloat16),
        value_sum.astype(jnp.bfloat16),
    )


def solution(mesh):
    in_specs = (
        P(("mem", "kvh", "row"), None),
        P(("mem", "kvh", "row"), None),
        P("mem", "kvh"),
        P("mem", "kvh"),
        P(None, "row"),
        P(),
    )
    out_specs = (
        P(("mem", "kvh", "row"), None),
        P(("mem", "kvh", "row"), None),
        P("mem", "kvh"),
        P("mem", "kvh"),
    )
    return jax.shard_map(
        per_device, mesh=mesh, in_specs=in_specs, out_specs=out_specs, check_vma=False
    )
```

profile of v0, /device:TPU:1, one launch (start us, length us, event | category | flops | bytes accessed | tf_op | source)
XLA Modules:
  0.0 531.2 jit_solution(9227071309435036342)
XLA Ops:
  7.2 12.4 %all_to_all.100 = bf16[2,4,2048]{2,0,1:T(2,128)(2,1)S(1)} all-to-all(bf16[2,4,2048]{2,0,1:T(2,128)(2,1)} %bitcast.198), channel_id=1, replica_groups=mesh['mem'=32,'kvh'=4,'row'=4] {'kvh'}, dimensions={1} | all-to-all | bytes 65536 | tf_op jit(solution)/shard_map/all_to_all | solution.py:59
  19.6 3.3 all-to-all-start
  23.0 4.4 all-to-all-done
  30.3 97.0 %all-gather.2.cloned.1.call-done = bf16[256,4096]{1,0:T(8,128)(2,1)} async-done(((bf16[8,4096]{1,0:T(8,128)(2,1)}), bf16[256,4096]{1,0:T(8,128)(2,1)}) %all-gather.2.cloned.1.call-update) | async-done | bytes 2097168 | tf_op jit(solution)/shard_map/all_gather | solution.py:17
  127.3 2.7 fusion.36
  131.9 50.9 %while.30 = (s32[]{:T(128)}, f32[256,2,8]{0,2,1:T(8,128)S(1)}, f32[256,2,8]{0,2,1:T(8,128)S(1)}, f32[256,2,8,128]{0,3,2,1:T(8,128)}, s32[6]{0:T(128)S(1)}, /*ind...) while((s32[]{:T(128)}, f32[256,2,8]{0,2,1:T(8,128)S(1)}, ...), condition=%wide.region_5.6_spmd.clone, body=%wide.region_2.5_spmd.clone.sunk | while | flops 276844544 | bytes 12191419 | solution.py:107
  144.1 3.7 bitcast_add_fusion.4
  152.8 3.7 bitcast_add_fusion.4
  161.6 3.7 bitcast_add_fusion.4
  170.3 3.7 bitcast_add_fusion.4
  179.1 3.7 bitcast_add_fusion.4
  185.6 4.4 all-to-all-start.3
  192.7 9.0 %all-to-all-done.3 = f32[32,1,128]{2,1,0:T(1,128)S(1)} async-done(((f32[32,1,128]{2,1,0:T(1,128)}), f32[32,1,128]{2,1,0:T(1,128)S(1)}, u32[]{:S(2)}, u32[]{:S(2)}) %all-to-all-start.3) | async-done | bytes 16416 | tf_op jit(solution)/shard_map/all_to_all | solution.py:118
  201.7 4.3 all-to-all-start.4
  208.0 9.8 %all-to-all-done.4 = f32[32,1,128]{2,1,0:T(1,128)S(1)} async-done(((f32[32,1,128]{2,1,0:T(1,128)}), f32[32,1,128]{2,1,0:T(1,128)S(1)}, u32[]{:S(2)}, u32[]{:S(2)}) %all-to-all-start.4) | async-done | bytes 16416 | tf_op jit(solution)/shard_map/all_to_all | solution.py:119
  218.4 4.4 all-to-all-start.2
  229.7 50.5 %all-to-all-done.2 = f32[32,8,2,8,128]{4,3,2,1,0:T(8,128)S(1)} async-done(((f32[32,8,2,8,128]{4,3,2,1,0:T(8,128)}), f32[32,8,2,8,128]{4,3,2,1,0:T(8,128)S(1)}, u32[]{:S(2)}, u32[]{:S(2)}) %all-to-all-start.2) | async-done | bytes 2097184 | tf_op jit(solution)/shard_map/all_to_all | solution.py:117
  281.3 50.5 %all_gather.7 = f32[256,4,8]{2,1,0:T(4,128)S(1)} all-gather(f32[8,4,8]{2,1,0:T(4,128)S(1)} %copy.109), channel_id=1, replica_groups=mesh['mem'=32,'kvh'=4,'row'=4] {'mem'}, dimensions={0}, use_global_device_ids=true | all-gather | bytes 33792 | tf_op jit(solution)/shard_map/all_gather | solution.py:17
  332.8 3.9 all-to-all-start.5
  336.7 87.4 %while.31 = (s32[]{:T(128)}, f32[256,2,8,128]{0,3,2,1:T(8,128)}, bf16[6,128,2,128]{3,1,2,0:T(8,128)(2,1)}, bf16[6,128,2,128]{3,1,2,0:T(8,128)(2,1)}, s32[6]{0:T(...) while((s32[]{:T(128)}, f32[256,2,8,128]{0,3,2,1:T(8,128)}, ...), condition=%wide.region_11.12_spmd.clone, body=%wide.region_10.11_spmd.clone.sunk | while | flops 676888576 | bytes 22776864 | solution.py:159
  357.9 3.4 bitcast_add_fusion.5
  372.7 3.4 bitcast_add_fusion.5
  387.6 3.4 bitcast_add_fusion.5
  402.4 3.4 bitcast_add_fusion.5
  417.2 3.4 bitcast_add_fusion.5
  426.9 4.5 all-to-all-start.8
  433.3 18.5 %all-to-all-done.8 = bf16[4,768,256]{2,1,0:T(8,128)(2,1)} async-done(((bf16[4,768,256]{2,1,0:T(8,128)(2,1)}), bf16[4,768,256]{2,1,0:T(8,128)(2,1)}, u32[]{:S(2)}, u32[]{:S(2)}) %all-to-all-start.8) | async-done | bytes 1572896 | tf_op jit(solution)/shard_map/all_to_all | solution.py:26
  451.9 8.9 %all-to-all-start.6 = ((bf16[32,8,2,8,128]{4,3,2,1,0:T(8,128)(2,1)}), bf16[32,8,2,8,128]{4,3,2,1,0:T(8,128)(2,1)S(1)}, u32[]{:S(2)}, u32[]{:S(2)}) async-start(bf16[32,8,2,8,128]{4,3,2,1,0:T(8,128)(2,1)} %bitcast.10), calls=%async_computation.6 | async-start | bytes 2097152 | tf_op jit(solution)/shard_map/all_to_all | solution.py:43
  462.3 28.9 %all-to-all-done.6 = bf16[32,8,2,8,128]{4,3,2,1,0:T(8,128)(2,1)S(1)} async-done(((bf16[32,8,2,8,128]{4,3,2,1,0:T(8,128)(2,1)}), bf16[32,8,2,8,128]{4,3,2,1,0:T(8,128)(2,1)S(1)}, u32[]{:S(2)}, u32[]{:S(2)}) %all-to-all-start.6) | async-done | bytes 1048608 | tf_op jit(solution)/shard_map/all_to_all | solution.py:43
  492.4 3.6 all-to-all-start.9
  496.8 17.7 %all-to-all-done.9 = bf16[4,768,256]{2,1,0:T(8,128)(2,1)S(1)} async-done(((bf16[4,768,256]{2,1,0:T(8,128)(2,1)}), bf16[4,768,256]{2,1,0:T(8,128)(2,1)S(1)}, u32[]{:S(2)}, u32[]{:S(2)}) %all-to-all-start.9) | async-done | bytes 1572896 | tf_op jit(solution)/shard_map/all_to_all | solution.py:26
  514.5 3.3 all-to-all-start.7
  (247 shorter events, 113.9 us)
Async XLA Ops:
  7.2 22.1 %copy-start.4 = (bf16[768,256]{1,0:T(8,128)(2,1)S(1)}, bf16[768,256]{1,0:T(8,128)(2,1)}, u32[]{:S(2)}) copy-start(bf16[768,256]{1,0:T(8,128)(2,1)} %param.13) | copy-start | bytes 1179652
  7.2 22.2 %copy-start.11 = (s32[96]{0:T(128)S(1)}, s32[96]{0:T(128)}, u32[]{:S(2)}) copy-start(s32[96]{0:T(128)} %param.15) | copy-start | bytes 1156
  7.2 22.6 %copy-start.10 = (s32[128,2]{0,1:T(2,128)S(1)}, s32[128,2]{0,1:T(2,128)}, u32[]{:S(2)}) copy-start(s32[128,2]{0,1:T(2,128)} %param.14) | copy-start | bytes 3076
  19.6 7.7 %all-to-all-start = ((bf16[2,4,2048]{2,0,1:T(2,128)(2,1)}), bf16[2,4,2048]{2,0,1:T(2,128)(2,1)S(1)}, u32[]{:S(2)}, u32[]{:S(2)}) async-start(bf16[2,4,2048]{2,0,1:T(2,128)(2,1)} %bitcast.199), calls=%async_computation | async-start | bytes 65536 | tf_op jit(solution)/shard_map/all_to_all | solution.py:58
  22.9 104.4 %all-gather.2.cloned.1.call-start = ((), (), s32[]{:S(2)}) async-start(), calls=%async_computation.10 | async-start | bytes 2162688 | tf_op jit(solution)/shard_map/all_gather | solution.py:17
  182.8 25.1 %copy-start.3 = (bf16[6,128,2,128]{3,2,1,0:T(2,128)(2,1)}, bf16[6,128,2,128]{3,2,1,0:T(2,128)(2,1)S(1)}, u32[]{:S(2)}) copy-start(bf16[6,128,2,128]{3,2,1,0:T(2,128)(2,1)S(1)} %get-tuple-element.573) | copy-start | bytes 1179652
  182.8 25.1 %copy-start.6 = (pred[256,6]{0,1:T(8,128)(4,1)}, pred[256,6]{0,1:T(8,128)(4,1)S(1)}, u32[]{:S(2)}) copy-start(pred[256,6]{0,1:T(8,128)(4,1)S(1)} %get-tuple-element.579) | copy-start | bytes 4612
  182.8 23.1 %copy-start.2 = (f32[256,2,8,128]{0,3,2,1:T(8,128)S(1)}, f32[256,2,8,128]{0,3,2,1:T(8,128)}, u32[]{:S(2)}) copy-start(f32[256,2,8,128]{0,3,2,1:T(8,128)} %get-tuple-element.117) | copy-start | bytes 6291460
  185.6 16.1 %all-to-all-start.3 = ((f32[32,1,128]{2,1,0:T(1,128)}), f32[32,1,128]{2,1,0:T(1,128)S(1)}, u32[]{:S(2)}, u32[]{:S(2)}) async-start(f32[32,1,128]{2,1,0:T(1,128)} %reshape.134), calls=%async_computation.3 | async-start | bytes 32768 | tf_op jit(solution)/shard_map/all_to_all | solution.py:118
  201.7 16.1 %all-to-all-start.4 = ((f32[32,1,128]{2,1,0:T(1,128)}), f32[32,1,128]{2,1,0:T(1,128)S(1)}, u32[]{:S(2)}, u32[]{:S(2)}) async-start(f32[32,1,128]{2,1,0:T(1,128)} %reshape.136), calls=%async_computation.4 | async-start | bytes 32768 | tf_op jit(solution)/shard_map/all_to_all | solution.py:119
  218.4 61.8 %all-to-all-start.2 = ((f32[32,8,2,8,128]{4,3,2,1,0:T(8,128)}), f32[32,8,2,8,128]{4,3,2,1,0:T(8,128)S(1)}, u32[]{:S(2)}, u32[]{:S(2)}) async-start(f32[32,8,2,8,128]{4,3,2,1,0:T(8,128)} %bitcast.186), calls=%async_computation.2 | async-start | bytes 4194304 | tf_op jit(solution)/shard_map/all_to_all | solution.py:117
  229.3 51.6 %copy-start.5 = (f32[8,2,8,128]{3,2,1,0:T(8,128)S(1)}, f32[8,2,8,128]{3,2,1,0:T(8,128)}, u32[]{:S(2)}) copy-start(f32[8,2,8,128]{3,2,1,0:T(8,128)} %reshape.123) | copy-start | bytes 196612
  332.8 92.7 %all-to-all-start.5 = ((bf16[4,2,2048]{2,1,0:T(2,128)(2,1)}), bf16[4,2,2048]{2,1,0:T(2,128)(2,1)}, u32[]{:S(2)}, u32[]{:S(2)}) async-start(bf16[4,2,2048]{2,1,0:T(2,128)(2,1)} %convert_element_type.60), calls=%async_computation.5 | async-start | bytes 65536 | tf_op jit(solution)/shard_map/all_to_all | solution.py:173
  336.7 2.8 copy-start.12
  336.8 6.2 %copy-start.8 = (f32[256,2,8]{0,2,1:T(8,128)}, f32[256,2,8]{0,2,1:T(8,128)S(1)}, u32[]{:S(2)}) copy-start(f32[256,2,8]{0,2,1:T(8,128)S(1)} %get-tuple-element.549) | copy-start | bytes 49156 | tf_op jit(solution)/shard_map/while
  346.5 2.4 copy-start
  350.0 2.8 copy-start.12
  350.0 6.2 %copy-start.8 = (f32[256,2,8]{0,2,1:T(8,128)}, f32[256,2,8]{0,2,1:T(8,128)S(1)}, u32[]{:S(2)}) copy-start(f32[256,2,8]{0,2,1:T(8,128)S(1)} %get-tuple-element.549) | copy-start | bytes 49156 | tf_op jit(solution)/shard_map/while
  364.8 2.8 copy-start.12
  364.8 6.2 %copy-start.8 = (f32[256,2,8]{0,2,1:T(8,128)}, f32[256,2,8]{0,2,1:T(8,128)S(1)}, u32[]{:S(2)}) copy-start(f32[256,2,8]{0,2,1:T(8,128)S(1)} %get-tuple-element.549) | copy-start | bytes 49156 | tf_op jit(solution)/shard_map/while
  376.2 2.4 copy-start
  379.6 2.8 copy-start.12
  379.6 6.2 %copy-start.8 = (f32[256,2,8]{0,2,1:T(8,128)}, f32[256,2,8]{0,2,1:T(8,128)S(1)}, u32[]{:S(2)}) copy-start(f32[256,2,8]{0,2,1:T(8,128)S(1)} %get-tuple-element.549) | copy-start | bytes 49156 | tf_op jit(solution)/shard_map/while
  394.5 2.8 copy-start.12
  394.5 6.2 %copy-start.8 = (f32[256,2,8]{0,2,1:T(8,128)}, f32[256,2,8]{0,2,1:T(8,128)S(1)}, u32[]{:S(2)}) copy-start(f32[256,2,8]{0,2,1:T(8,128)S(1)} %get-tuple-element.549) | copy-start | bytes 49156 | tf_op jit(solution)/shard_map/while
  409.3 2.8 copy-start.12
  409.3 6.2 %copy-start.8 = (f32[256,2,8]{0,2,1:T(8,128)}, f32[256,2,8]{0,2,1:T(8,128)S(1)}, u32[]{:S(2)}) copy-start(f32[256,2,8]{0,2,1:T(8,128)S(1)} %get-tuple-element.549) | copy-start | bytes 49156 | tf_op jit(solution)/shard_map/while
  425.6 5.8 %copy-start.1 = (f32[256,2,8,128]{0,3,2,1:T(8,128)S(1)}, f32[256,2,8,128]{0,3,2,1:T(8,128)}, u32[]{:S(2)}) copy-start(f32[256,2,8,128]{0,3,2,1:T(8,128)} %get-tuple-element.120) | copy-start | bytes 6291460
  426.9 25.0 %all-to-all-start.8 = ((bf16[4,768,256]{2,1,0:T(8,128)(2,1)}), bf16[4,768,256]{2,1,0:T(8,128)(2,1)}, u32[]{:S(2)}, u32[]{:S(2)}) async-start(bf16[4,768,256]{2,1,0:T(8,128)(2,1)} %broadcast_in_dim.79), calls=%async_computation.8 | async-start | bytes 3145728 | tf_op jit(solution)/shard_map/all_to_all | solution.py:26
  451.9 39.3 %all-to-all-start.6 = ((bf16[32,8,2,8,128]{4,3,2,1,0:T(8,128)(2,1)}), bf16[32,8,2,8,128]{4,3,2,1,0:T(8,128)(2,1)S(1)}, u32[]{:S(2)}, u32[]{:S(2)}) async-start(bf16[32,8,2,8,128]{4,3,2,1,0:T(8,128)(2,1)} %bitcast.10), calls=%async_computation.6 | async-start | bytes 2097152 | tf_op jit(solution)/shard_map/all_to_all | solution.py:43
  492.4 22.1 %all-to-all-start.9 = ((bf16[4,768,256]{2,1,0:T(8,128)(2,1)}), bf16[4,768,256]{2,1,0:T(8,128)(2,1)S(1)}, u32[]{:S(2)}, u32[]{:S(2)}) async-start(bf16[4,768,256]{2,1,0:T(8,128)(2,1)} %broadcast_in_dim.80), calls=%async_computation.9 | async-start | bytes 3145728 | tf_op jit(solution)/shard_map/all_to_all | solution.py:26
  514.5 7.8 %all-to-all-start.7 = ((bf16[4,2,2048]{2,1,0:T(2,128)(2,1)}), bf16[4,2,2048]{2,1,0:T(2,128)(2,1)S(1)}, u32[]{:S(2)}, u32[]{:S(2)}) async-start(bf16[4,2,2048]{2,1,0:T(2,128)(2,1)} %convert_element_type.64), calls=%async_computation.7 | async-start | bytes 65536 | tf_op jit(solution)/shard_map/all_to_all | solution.py:174
  (17 other events, 23.3 us)
Sparse Core Ops, SparseCore 0:
  28.2 99.0 all-gather.1
where the time goes:
time: 540 us; the launch traced here: 531 us
  waiting for transfers between devices  237 us (44%)
  matrix products  92 us (17%)
  blocking collectives  63 us (12%)
  local copies, waits for them, and re-layouts  48.3 us (9%)
  starting transfers between devices  40.6 us (8%)
  loops' own time  24.8 us (5%)
  between operations  14.4 us (3%)
  other arithmetic  11.2 us (2%)
    all_gather x1, waiting for transfers between devices, in_one_piece(): result, at, outs = (lax.all_gather(both, axis, axis=dim, tiled=True), 0, [])  97 us
    all_to_all x1, waiting for transfers between devices, per_device(): lax.all_to_all(sent[0], 'mem', split_axis=0, concat_axis=0, tiled=True)  50.5 us
    all_gather x1, blocking collectives, in_one_piece(): result, at, outs = (lax.all_gather(both, axis, axis=dim, tiled=True), 0, [])  50.5 us
    all_to_all x2, waiting for transfers between devices, sent_to_all(): lax.all_to_all(jnp.broadcast_to(array[None], (count, *array.shape)), axis...  36.3 us
    all_to_all x1, waiting for transfers between devices, sent_and_summed(): lax.all_to_all(pieces, axis, split_axis=0, concat_axis=0, tiled=True)  28.9 us
    dot_general x12, matrix products, frame_scores(): jnp.einsum('rghd,jgd->rghj', query_four, key_block, preferred_element_typ...  21.3 us
    dot_general x6, matrix products, forward_step(): jnp.einsum('rghj,jgd->rghd', weight.astype(jnp.bfloat16), value_block, pr...  20.9 us
    dot_general x6, matrix products, backward_step(): jnp.einsum('rghj,jgd->rghd', score_grad, key_block, preferred_element_typ...  19.1 us
  transfers between devices with their start and end apart: 10, of which 9 were waited for; matrix products, arithmetic and copies ran while one was open for 18% of the time, Pallas kernels for 0%

commit v1 on v0

v1 whole, which is shorter than its diff:
```python
import functools

import jax
import jax.numpy as jnp
from jax import lax
from jax.experimental import pallas as pl
from jax.experimental.pallas import tpu as pltpu
from jax.sharding import PartitionSpec as P

HEADS = 64
KV = 8
D = 128
GROUP = HEADS // KV
ROWS = 2
NY = 8
NZH = 2
NK = 4
NC = 2
NX = 4
COL = NZH * NK * NC
CHIPS = NZH * NY
PIECE = ROWS * GROUP
CH = COL * PIECE
TOK = 768
TOKENS = NC * TOK
TB = 256
NB = TOKENS // TB
QT = TOKENS // NX
FRAME = 128
SCALE = D ** (-0.5)
LOG2E = 1.4426950408889634
CS = SCALE * LOG2E
NEG = -1e30
MESH = pl.DeviceIdType.MESH
BF = jnp.bfloat16
F32 = jnp.float32


def dot_nt(a, b):
    return lax.dot_general(a, b, (((1,), (1,)), ((), ())), preferred_element_type=F32)


def dot_nn(a, b):
    return lax.dot_general(a, b, (((1,), (0,)), ((), ())), preferred_element_type=F32)


def kernel(
    xin, keys, values, nvis,
    fin, kvout,
    buf, kbuf, vbuf, kt, vt, wbuf, dpbuf, mst, stats,
    osend, orecv, dqsend, dqrecv, dk, dv, rssend, rsrecv, agsrc, fsend, frecv,
    a_send, a_recv, kv_send, kv_recv, kv_loc, r_send, r_recv, o_send, o_recv, q_send, q_recv,
    s_send, s_recv, rs_send, rs_recv, f_send, f_recv, ag_send, ag_recv,
):
    m = lax.axis_index("mem")
    k = lax.axis_index("kvh")
    x = lax.axis_index("row")
    c = lax.rem(m, 2)
    n = lax.div(m, 2)
    y = lax.rem(n, NY)
    zh = lax.div(n, NY)
    s = (zh * NK + k) * NC + c

    def column(t):
        zz = lax.div(t, 2)
        return ((lax.div(zz, NK) * NY + y) * 2 + lax.rem(t, 2), lax.rem(zz, NK), x)

    def chip(t):
        return (t * 2 + c, k, x)

    def at_y(t):
        return ((zh * NY + t) * 2 + c, k, x)

    def at_x(t, core):
        return (n * 2 + core, k, t)

    def remote(src, dst, ss, rs, dev):
        return pltpu.make_async_remote_copy(
            src_ref=src, dst_ref=dst, send_sem=ss, recv_sem=rs, device_id=dev, device_id_type=MESH
        )

    other = 1 - c
    mine_cols = pl.ds(pl.multiple_of(c * D, D), D)
    other_cols = pl.ds(pl.multiple_of(other * D, D), D)
    loc_k = pltpu.make_async_copy(keys.at[:, mine_cols], kbuf.at[c], kv_loc.at[0])
    loc_v = pltpu.make_async_copy(values.at[:, mine_cols], vbuf.at[c], kv_loc.at[1])
    loc_k.start()
    loc_v.start()

    barrier = pltpu.get_barrier_semaphore()

    def greet_col(j, _):
        pl.semaphore_signal(barrier, inc=1, device_id=column(lax.rem(s + j, COL)), device_id_type=MESH)
        return 0

    def greet_chip(j, _):
        pl.semaphore_signal(barrier, inc=1, device_id=chip(lax.rem(n + j, CHIPS)), device_id_type=MESH)
        return 0

    lax.fori_loop(1, COL, greet_col, 0)
    lax.fori_loop(1, CHIPS, greet_chip, 0)
    for j in range(1, NX):
        for core in range(2):
            pl.semaphore_signal(
                barrier, inc=1, device_id=at_x(lax.rem(x + j, NX), core), device_id_type=MESH
            )
    pl.semaphore_wait(barrier, (COL - 1) + (CHIPS - 1) + 2 * (NX - 1))

    def a_copy(src_s, dst_s, dev):
        return remote(
            xin.at[lax.rem(dst_s, KV)], buf.at[y, :, src_s], a_send.at[dst_s], a_recv.at[src_s], dev
        )

    def a_start(j, _):
        t = lax.rem(s + j, COL)
        a_copy(s, t, column(t)).start()
        return 0

    lax.fori_loop(1, COL, a_start, 0)
    kcopy = remote(keys.at[:, other_cols], kbuf.at[c], kv_send.at[0], kv_recv.at[0], (n * 2 + other, k, x))
    vcopy = remote(values.at[:, other_cols], vbuf.at[c], kv_send.at[1], kv_recv.at[1], (n * 2 + other, k, x))
    kcopy.start()
    vcopy.start()
    own = xin[lax.rem(s, KV)]
    buf[y, 0, s] = own[0]
    buf[y, 1, s] = own[1]
    loc_k.wait()
    loc_v.wait()

    def a_wait(j, _):
        t = lax.rem(s + j, COL)
        a_copy(t, s, column(t)).wait_recv()
        return 0

    lax.fori_loop(1, COL, a_wait, 0)

    right = at_y(lax.rem(y + 1, NY))
    left = at_y(lax.rem(y + NY - 1, NY))

    def ring(way, kind, t):
        g = lax.rem(y + NY - t, NY) if way == 0 else lax.rem(y + t, NY)
        ref = buf.at[g, kind]
        return remote(ref, ref, r_send.at[way, kind, t], r_recv.at[way, kind, t], right if way == 0 else left)

    def ring_arrival(way, kind, t):
        g = lax.rem(y + NY - 1 - t, NY) if way == 0 else lax.rem(y + 1 + t, NY)
        ref = buf.at[g, kind]
        return remote(ref, ref, r_send.at[way, kind, t], r_recv.at[way, kind, t], right if way == 0 else left)

    for kind in range(2):
        for way in range(2):
            ring(way, kind, 0).start()

    kcopy.wait_recv()
    vcopy.wait_recv()
    for h in range(2):
        kt[:, h * TOK:(h + 1) * TOK] = kbuf[h].T
        vt[:, h * TOK:(h + 1) * TOK] = vbuf[h].T

    def chunk_at(i):
        half = lax.div(i + 1, 2)
        return jnp.where(lax.rem(i, 2) == 1, lax.rem(y + NY - half, NY), lax.rem(y + half, NY))

    def token_block(ref, b):
        h = b * TB // TOK
        return ref[h, b * TB - h * TOK:(b + 1) * TB - h * TOK]

    def forward(i, _):
        @pl.when(lax.rem(i, 2) == 1)
        def _():
            t = lax.div(i - 1, 2)
            for kind in range(2):
                for way in range(2):
                    last_too = kind == way

                    if last_too:
                        ring_arrival(way, kind, t).wait_recv()

                        @pl.when(t < 3)
                        def _():
                            ring(way, kind, t + 1).start()
                    else:
                        @pl.when(t < 3)
                        def _():
                            ring_arrival(way, kind, t).wait_recv()

                        @pl.when(t < 2)
                        def _():
                            ring(way, kind, t + 1).start()

        g = chunk_at(i)
        q = buf[g, 0].reshape(CH, D)
        d = buf[g, 1].reshape(CH, D)
        nv = nvis[g]
        top = jnp.full((1, CH), NEG, F32)
        for b in range(NB):
            sc = dot_nt(token_block(kbuf, b), q)
            wbuf[g, b] = sc
            for u in range(TB // FRAME):
                part = jnp.max(sc[u * FRAME:(u + 1) * FRAME], axis=0, keepdims=True)
                top = jnp.maximum(top, jnp.where(nv > b * (TB // FRAME) + u, part, NEG))
        msc = top * CS
        total = jnp.zeros((1, CH), F32)
        dsum = jnp.zeros((1, CH), F32)
        acc = jnp.zeros((D, CH), F32)
        for b in range(NB):
            dp = dot_nt(token_block(vbuf, b), d)
            dpbuf[g, b] = dp
            ws = []
            for u in range(TB // FRAME):
                bias = jnp.where(nv > b * (TB // FRAME) + u, -msc, NEG)
                ws.append(jnp.exp2(wbuf[g, b, u * FRAME:(u + 1) * FRAME] * CS + bias))
            w = jnp.concatenate(ws, axis=0)
            wbuf[g, b] = w
            total = total + jnp.sum(w, axis=0, keepdims=True)
            dsum = dsum + jnp.sum(w * dp, axis=0, keepdims=True)
            acc = acc + dot_nn(vt[:, b * TB:(b + 1) * TB], w.astype(BF))
        seen = nv > 0
        inv = jnp.where(seen, 1.0 / jnp.where(seen, total, 1.0), 0.0)
        stats[n, g, 0] = jnp.where(seen, msc + jnp.log2(jnp.where(seen, total, 1.0)), NEG)
        stats[n, g, 1] = dsum * inv
        mst[g] = msc
        out = (acc * inv).astype(BF)

        def s_start(j, _):
            t = lax.rem(n + j, CHIPS)
            ref = stats.at[n, g]
            remote(ref, ref, s_send.at[t], s_recv.at[n], chip(t)).start()
            return 0

        lax.fori_loop(1, CHIPS, s_start, 0)

        @pl.when(g == y)
        def _():
            orecv[y] = out

        @pl.when(g != y)
        def _():
            osend[g] = out
            remote(osend.at[g], orecv.at[y], o_send.at[g], o_recv.at[y], at_y(g)).start()

        return 0

    lax.fori_loop(0, NY, forward, 0)

    def s_wait(j, _):
        t = lax.rem(n + j, CHIPS)
        ref = stats.at[t]
        remote(ref, ref, s_send.at[t], s_recv.at[t], chip(t)).wait_recv()
        return 0

    lax.fori_loop(1, CHIPS, s_wait, 0)

    def whole_stats(g):
        peak = stats[0, g, 0]
        for t in range(1, CHIPS):
            peak = jnp.maximum(peak, stats[t, g, 0])
        mass = jnp.zeros((1, CH), F32)
        dsum = jnp.zeros((1, CH), F32)
        for t in range(CHIPS):
            e = jnp.exp2(stats[t, g, 0] - peak)
            mass = mass + e
            dsum = dsum + e * stats[t, g, 1]
        return peak + jnp.log2(mass), dsum / mass

    dk[...] = jnp.zeros_like(dk)
    dv[...] = jnp.zeros_like(dv)

    def backward(i, _):
        g = chunk_at(NY - 1 - i)
        q = buf[g, 0].reshape(CH, D)
        d = buf[g, 1].reshape(CH, D)
        lse, delta = whole_stats(g)
        f = jnp.exp2(mst[g] - lse)
        acc = jnp.zeros((D, CH), F32)
        for b in range(NB):
            p = wbuf[g, b] * f
            ds = (p * (dpbuf[g, b] - delta)).astype(BF)
            rows = slice(b * TB, (b + 1) * TB)
            dv[rows] = dv[rows] + dot_nn(p.astype(BF), d)
            dk[rows] = dk[rows] + dot_nn(ds, q)
            acc = acc + dot_nn(kt[:, rows], ds)
        out = (acc * SCALE).astype(BF)

        @pl.when(g == y)
        def _():
            dqrecv[y] = out

        @pl.when(g != y)
        def _():
            dqsend[g] = out
            remote(dqsend.at[g], dqrecv.at[y], q_send.at[g], q_recv.at[y], at_y(g)).start()

        return 0

    lax.fori_loop(0, NY, backward, 0)

    def rs_copy(src, dst):
        return remote(rssend.at[dst], rsrecv.at[src], rs_send.at[dst], rs_recv.at[src], at_x(dst, c))

    for t in range(NX):
        rssend[t, 0] = (dk[t * QT:(t + 1) * QT] * SCALE).astype(BF)
        rssend[t, 1] = dv[t * QT:(t + 1) * QT].astype(BF)
    for j in (2, 1, 3):
        rs_copy(x, lax.rem(x + j, NX)).start()

    def o_wait(j, _):
        t = lax.rem(y + j, NY)
        remote(osend.at[t], orecv.at[t], o_send.at[t], o_recv.at[t], at_y(t)).wait_recv()
        return 0

    lax.fori_loop(1, NY, o_wait, 0)
    lse, _ = whole_stats(y)
    acc = jnp.zeros((D, CH), F32)
    for t in range(NY):
        acc = acc + orecv[t].astype(F32) * jnp.exp2(stats[zh * NY + t, y, 0] - lse)
    fsend[0] = acc.T.astype(BF).reshape(COL, PIECE, D)

    def q_wait(j, _):
        t = lax.rem(y + j, NY)
        remote(dqsend.at[t], dqrecv.at[t], q_send.at[t], q_recv.at[t], at_y(t)).wait_recv()
        return 0

    lax.fori_loop(1, NY, q_wait, 0)
    acc = jnp.zeros((D, CH), F32)
    for t in range(NY):
        acc = acc + dqrecv[t].astype(F32)
    fsend[1] = acc.T.astype(BF).reshape(COL, PIECE, D)

    def f_copy(src, dst):
        return remote(fsend.at[:, dst], frecv.at[src], f_send.at[dst], f_recv.at[src], column(dst))

    def f_start(j, _):
        f_copy(s, lax.rem(s + j, COL)).start()
        return 0

    lax.fori_loop(1, COL, f_start, 0)
    frecv[s, 0] = fsend[0, s]
    frecv[s, 1] = fsend[1, s]

    for j in range(1, NX):
        rs_copy(lax.rem(x + j, NX), x).wait_recv()
    for a in range(2):
        acc = rssend[x, a].astype(F32)
        for j in range(1, NX):
            acc = acc + rsrecv[lax.rem(x + j, NX), a].astype(F32)
        agsrc[a] = acc.astype(BF)

    core = lax.div(x, 2)
    part = lax.rem(x, 2)

    def ag_copy(t):
        return remote(
            agsrc, kvout.at[:, part, c], ag_send.at[t], ag_recv.at[part, c], at_x(t, core)
        )

    for j in (2, 1, 3):
        ag_copy(lax.rem(x + j, NX)).start()

    @pl.when(core != c)
    def _():
        ag_copy(x).start()

    @pl.when(core == c)
    def _():
        kvout[0, part, c] = agsrc[0]
        kvout[1, part, c] = agsrc[1]

    def f_wait(j, _):
        f_copy(lax.rem(s + j, COL), s).wait_recv()
        return 0

    lax.fori_loop(1, COL, f_wait, 0)
    for h in range(KV):
        for a in range(2):
            fin[a, h] = (frecv[h, a].astype(F32) + frecv[KV + h, a].astype(F32)).astype(BF)

    for pp in range(2):
        for hh in range(2):
            itself = jnp.logical_and(c * 2 + pp == x, hh == c)

            @pl.when(jnp.logical_not(itself))
            def _():
                remote(
                    agsrc, kvout.at[:, pp, hh], ag_send.at[0], ag_recv.at[pp, hh], at_x(x, other)
                ).wait_recv()

    def col_sent(j, _):
        t = lax.rem(s + j, COL)
        a_copy(s, t, column(t)).wait_send()
        f_copy(s, t).wait_send()
        return 0

    lax.fori_loop(1, COL, col_sent, 0)
    kcopy.wait_send()
    vcopy.wait_send()
    for kind in range(2):
        for way in range(2):
            for t in range(4 if kind == way else 3):
                ring(way, kind, t).wait_send()

    def y_sent(j, _):
        t = lax.rem(y + j, NY)
        remote(osend.at[t], orecv.at[y], o_send.at[t], o_recv.at[y], at_y(t)).wait_send()
        remote(dqsend.at[t], dqrecv.at[y], q_send.at[t], q_recv.at[y], at_y(t)).wait_send()
        return 0

    lax.fori_loop(1, NY, y_sent, 0)

    def s_sent(j, _):
        t = lax.rem(n + j, CHIPS)
        ref = stats.at[n]
        remote(ref, ref, s_send.at[t], s_recv.at[n], chip(t)).wait_send()
        return 0

    lax.fori_loop(1, CHIPS, s_sent, 0)
    for j in range(1, NX):
        rs_copy(x, lax.rem(x + j, NX)).wait_send()
        ag_copy(lax.rem(x + j, NX)).wait_send()

    @pl.when(core != c)
    def _():
        ag_copy(x).wait_send()


def per_device(queries, output_gradient, keys, values, text_video, video_blocks):
    n = lax.axis_index("mem") // 2
    both = jnp.stack([queries, output_gradient])
    xin = both.reshape(2, ROWS, KV, GROUP, D).transpose(2, 0, 1, 3, 4).reshape(KV, 2, PIECE, D)
    ids = jnp.arange(video_blocks.shape[0], dtype=jnp.int32)
    ends = jnp.sum(jnp.where(ids <= text_video[..., None], video_blocks, 0), axis=-1)
    frames = TOKENS // FRAME
    seen = jnp.clip(ends - n * frames, 0, frames)
    seen = seen.reshape(NZH, NY, NC, NK, ROWS).transpose(1, 0, 3, 2, 4)
    nvis = jnp.broadcast_to(seen[..., None], (NY, NZH, NK, NC, ROWS, GROUP)).reshape(NY, 1, CH)

    vm = pl.BlockSpec(memory_space=pltpu.VMEM)
    hbm = pl.BlockSpec(memory_space=pl.ANY)
    dma = pltpu.SemaphoreType.DMA
    fin, kvout = pl.pallas_call(
        kernel,
        name="attention_step",
        out_shape=(
            jax.ShapeDtypeStruct((2, KV, PIECE, D), BF),
            jax.ShapeDtypeStruct((2, 2, 2, QT, D), BF),
        ),
        in_specs=[vm, hbm, hbm, vm],
        out_specs=(vm, vm),
        scratch_shapes=[
            pltpu.VMEM((NY, 2, COL, PIECE, D), BF),
            pltpu.VMEM((NC, TOK, D), BF),
            pltpu.VMEM((NC, TOK, D), BF),
            pltpu.VMEM((D, TOKENS), BF),
            pltpu.VMEM((D, TOKENS), BF),
            pltpu.VMEM((NY, NB, TB, CH), F32),
            pltpu.VMEM((NY, NB, TB, CH), F32),
            pltpu.VMEM((NY, 1, CH), F32),
            pltpu.VMEM((CHIPS, NY, 2, 1, CH), F32),
            pltpu.VMEM((NY, D, CH), BF),
            pltpu.VMEM((NY, D, CH), BF),
            pltpu.VMEM((NY, D, CH), BF),
            pltpu.VMEM((NY, D, CH), BF),
            pltpu.VMEM((TOKENS, D), F32),
            pltpu.VMEM((TOKENS, D), F32),
            pltpu.VMEM((NX, 2, QT, D), BF),
            pltpu.VMEM((NX, 2, QT, D), BF),
            pltpu.VMEM((2, QT, D), BF),
            pltpu.VMEM((2, COL, PIECE, D), BF),
            pltpu.VMEM((COL, 2, PIECE, D), BF),
            dma((COL,)), dma((COL,)),
            dma((2,)), dma((2,)), dma((2,)),
            dma((2, 2, 4)), dma((2, 2, 4)),
            dma((NY,)), dma((NY,)), dma((NY,)), dma((NY,)),
            dma((CHIPS,)), dma((CHIPS,)),
            dma((NX,)), dma((NX,)),
            dma((COL,)), dma((COL,)),
            dma((NX,)), dma((2, 2)),
        ],
        compiler_params=pltpu.CompilerParams(
            collective_id=0, has_side_effects=True, vmem_limit_bytes=56 * 1024 * 1024
        ),
    )(xin, keys, values, nvis)
    out = fin.reshape(2, KV, ROWS, GROUP, D).transpose(0, 2, 1, 3, 4).reshape(2, ROWS, HEADS * D)
    grads = kvout.transpose(0, 1, 3, 2, 4).reshape(2, TOK, 2 * D)
    return out[0], out[1], grads[0], grads[1]


def solution(mesh):
    in_specs = (
        P(("mem", "kvh", "row"), None),
        P(("mem", "kvh", "row"), None),
        P("mem", "kvh"),
        P("mem", "kvh"),
        P(None, "row"),
        P(),
    )
    out_specs = (
        P(("mem", "kvh", "row"), None),
        P(("mem", "kvh", "row"), None),
        P("mem", "kvh"),
        P("mem", "kvh"),
    )
    return jax.shard_map(
        per_device, mesh=mesh, in_specs=in_specs, out_specs=out_specs, check_vma=False
    )
```

time: 540 us -> 92 us (0.17); the launches traced: 531 us -> 91.7 us
  waiting for transfers between devices: 237 us -> 0 us
  matrix products: 92 us -> 0 us
  Pallas kernels: 0 us -> 83.2 us
  blocking collectives: 63 us -> 0 us
  local copies, waits for them, and re-layouts: 48.3 us -> 7.02 us
  starting transfers between devices: 40.6 us -> 0 us
  loops' own time: 24.8 us -> 0 us
  between operations: 14.4 us -> 0.74 us
  other arithmetic: 11.2 us -> 0.74 us
    all_to_all x9 -> x0, waiting for transfers between devices: 140 us -> none  [the longest x1 50.5 us: per_device(): lax.all_to_all(sent[0], 'mem', split_axis=0, concat_axis=0, tiled=True)]
    all_gather x1 -> x0, waiting for transfers between devices: 97 us -> none  [in_one_piece(): result, at, outs = (lax.all_gather(both, axis, axis=dim, tiled=True), 0, [])]
    dot_general x42 -> x0, matrix products: 92 us -> none  [the longest x12 21.3 us: frame_scores(): jnp.einsum('rghd,jgd->rghj', query_four, key_block, preferred_element_typ...]
    pallas_call x0 -> x1, Pallas kernels: none -> 83.2 us  [per_device(): pl.pallas_call(kernel, name='attention_step', out_shape=(jax.ShapeDtypeSt...]
    all_gather x1 -> x0, blocking collectives: 50.5 us -> none  [in_one_piece(): result, at, outs = (lax.all_gather(both, axis, axis=dim, tiled=True), 0, [])]
    all_to_all x9 -> x0, starting transfers between devices: 40.6 us -> none  [the longest x1 8.9 us: sent_and_summed(): lax.all_to_all(pieces, axis, split_axis=0, concat_axis=0, tiled=True)]
    another operation x2 -> x0, loops' own time: 24.8 us -> none  [the longest x1 12.8 us: per_device(): lax.scan(backward_step, jnp.zeros(stat_shape + (HEAD_WIDTH,), jnp.float32...]
    dynamic_slice x42 -> x0, local copies, waits for them, and re-layouts: 18.2 us -> none  [the longest x12 7.48 us: per_device(): lax.scan(forward_step, start_state, frame_ids)]
  transfers between devices with their start and end apart: 10 -> 0, of which waited for: 9 -> 0; matrix products, arithmetic and copies ran while one was open for 18% -> 0% of each run, Pallas kernels for 0% -> 0%
where the time goes in v1:
time: 92 us; the launch traced here: 91.7 us
  Pallas kernels  83.2 us (90%)
  local copies, waits for them, and re-layouts  7.02 us (8%)
    pallas_call x1, Pallas kernels, per_device(): pl.pallas_call(kernel, name='attention_step', out_shape=(jax.ShapeDtypeSt...  83.2 us
    unnamed x12, local copies, waits for them, and re-layouts  2.32 us
    slice x6, local copies, waits for them, and re-layouts, per_device(): return (out[0], out[1], grads[0], grads[1])  2 us

profile of v1, /device:TPU:1, one launch (start us, length us, event | category | flops | bytes accessed | tf_op | source)
XLA Modules:
  0.0 91.7 jit_solution(460620364983871596)
XLA Ops:
  0.6 0.0 copy-start.3
  0.7 0.0 copy-start.4
  0.7 0.7 copy-done.3
  1.3 0.0 copy-done.4
  1.3 0.1 select_reduce_fusion
  1.4 0.1 min.12
  1.6 0.3 copy.25
  1.9 0.2 broadcast_in_dim.18
  2.1 0.0 copy-start.1
  2.1 0.0 copy-start.2
  2.1 0.8 reshape.42.nvis
  2.9 0.0 copy-done.1
  2.9 0.0 copy-done.2
  2.9 0.6 copy_bitcast_fusion.2.xin
  3.6 83.2 %attention_step.1 = (bf16[2,8,16,128]{3,2,1,0:T(8,128)(2,1)}, bf16[2,2,2,384,128]{4,3,2,1,0:T(8,128)(2,1)}) custom-call(bf16[8,2,16,128]{3,2,1,0:T(8,128)(2,1)} %copy_bitcast_fusion.2.xin, bf16[768,256]{1,0:T(8,128)(2,1)} %keys.1, bf16[768,256]{1,0:T(8,128)(2,1)} %values.1, s32[8,1,256]{2,1,0:T(1,128)} %reshape.42.nvis), custom_call_target="tpu_custom_call" | custom-call | tf_op jit(solution)/shard_map/attention_step/pallas_call | solution.py:440
  86.8 1.2 %fusion = (bf16[1,2,384,2,128]{4,2,3,1,0:T(8,128)(2,1)S(1)}, bf16[1,2,384,2,128]{4,2,3,1,0:T(8,128)(2,1)S(1)}) fusion(bf16[2,2,384,2,128]{4,2,3,1,0:T(8,128)(2,1)} %bitcast.35), kind=kLoop, calls=%fused_computation.9 | loop fusion | bytes 1572864 | tf_op jit(solution)/shard_map/slice | solution.py:485
  88.0 0.4 copy.29
  88.4 0.0 copy-start
  88.4 0.8 copy.40
  89.2 0.0 copy-done
  89.2 0.6 squeeze.13
  89.9 0.6 squeeze.12
  90.5 0.4 copy.28
  90.9 0.8 copy.41
  (5 shorter events, 0.0 us)
Async XLA Ops:
  0.6 0.7 copy-start.3
  0.7 0.7 copy-start.4
  2.1 0.8 copy-start.1
  2.1 0.8 copy-start.2
  88.4 0.8 copy-start

commit v2 on v1

--- a/solution.py
+++ b/solution.py
@@ -23,7 +23,7 @@
 CH = COL * PIECE
 TOK = 768
 TOKENS = NC * TOK
-TB = 256
+TB = 384
 NB = TOKENS // TB
 QT = TOKENS // NX
 FRAME = 128
@@ -46,8 +46,8 @@
 
 def kernel(
     xin, keys, values, nvis,
-    fin, kvout,
-    buf, kbuf, vbuf, kt, vt, wbuf, dpbuf, mst, stats,
+    fin_o, fin_q, kout, vout,
+    buf, kbuf, vbuf, kt, vt, wbuf, dpbuf, dsbuf, mst, fst, dst, stats,
     osend, orecv, dqsend, dqrecv, dk, dv, rssend, rsrecv, agsrc, fsend, frecv,
     a_send, a_recv, kv_send, kv_recv, kv_loc, r_send, r_recv, o_send, o_recv, q_send, q_recv,
     s_send, s_recv, rs_send, rs_recv, f_send, f_recv, ag_send, ag_recv,
@@ -165,6 +165,16 @@
         h = b * TB // TOK
         return ref[h, b * TB - h * TOK:(b + 1) * TB - h * TOK]
 
+    def stats_out(i):
+        ref = stats.at[n, chunk_at(i)]
+
+        def s_start(j, _):
+            t = lax.rem(n + j, CHIPS)
+            remote(ref, ref, s_send.at[t], s_recv.at[n], chip(t)).start()
+            return 0
+
+        lax.fori_loop(1, CHIPS, s_start, 0)
+
     def forward(i, _):
         @pl.when(lax.rem(i, 2) == 1)
         def _():
@@ -187,6 +197,14 @@
                         @pl.when(t < 2)
                         def _():
                             ring(way, kind, t + 1).start()
+
+        @pl.when(i == 5)
+        def _():
+            def early(e, _):
+                stats_out(e)
+                return 0
+
+            lax.fori_loop(0, 5, early, 0)
 
         g = chunk_at(i)
         q = buf[g, 0].reshape(CH, D)
@@ -222,26 +240,23 @@
         mst[g] = msc
         out = (acc * inv).astype(BF)
 
-        def s_start(j, _):
-            t = lax.rem(n + j, CHIPS)
-            ref = stats.at[n, g]
-            remote(ref, ref, s_send.at[t], s_recv.at[n], chip(t)).start()
-            return 0
-
-        lax.fori_loop(1, CHIPS, s_start, 0)
-
-        @pl.when(g == y)
+        osend[g] = out
+
+        @pl.when(i >= 5)
         def _():
-            orecv[y] = out
-
-        @pl.when(g != y)
-        def _():
-            osend[g] = out
-            remote(osend.at[g], orecv.at[y], o_send.at[g], o_recv.at[y], at_y(g)).start()
+            stats_out(i)
 
         return 0
 
     lax.fori_loop(0, NY, forward, 0)
+
+    def o_start(j, _):
+        g = chunk_at(NY - 1 - j)
+        remote(osend.at[g], orecv.at[y], o_send.at[g], o_recv.at[y], at_y(g)).start()
+        return 0
+
+    lax.fori_loop(0, NY - 1, o_start, 0)
+    orecv[y] = osend[y]
 
     def s_wait(j, _):
         t = lax.rem(n + j, CHIPS)
@@ -263,24 +278,45 @@
             dsum = dsum + e * stats[t, g, 1]
         return peak + jnp.log2(mass), dsum / mass
 
-    dk[...] = jnp.zeros_like(dk)
-    dv[...] = jnp.zeros_like(dv)
-
-    def backward(i, _):
+    def prepare(g, _):
+        lse, delta = whole_stats(g)
+        fst[g] = jnp.exp2(mst[g] - lse)
+        dst[g] = delta
+        return 0
+
+    lax.fori_loop(0, NY, prepare, 0)
+
+    def rs_copy(src, to):
+        return remote(rssend.at[to], rsrecv.at[src], rs_send.at[to], rs_recv.at[src], at_x(to, c))
+
+    for j in (2, 1, 3, 0):
+        b = lax.rem(x + j, NX)
+        dk[...] = jnp.zeros_like(dk)
+        dv[...] = jnp.zeros_like(dv)
+
+        def quarter(g, _):
+            q = buf[g, 0].reshape(CH, D)
+            d = buf[g, 1].reshape(CH, D)
+            f = fst[g]
+            delta = dst[g]
+            for u in range(QT // FRAME):
+                rows = slice(u * FRAME, (u + 1) * FRAME)
+                p = wbuf[g, b, rows] * f
+                ds = (p * (dpbuf[g, b, rows] - delta)).astype(BF)
+                dsbuf[g, b, rows] = ds
+                dv[rows] = dv[rows] + dot_nn(p.astype(BF), d)
+                dk[rows] = dk[rows] + dot_nn(ds, q)
+            return 0
+
+        lax.fori_loop(0, NY, quarter, 0)
+        rssend[b, 0] = (dk[...] * SCALE).astype(BF)
+        rssend[b, 1] = dv[...].astype(BF)
+        if j:
+            rs_copy(x, b).start()
+
+    def query_chunk(i, _):
         g = chunk_at(NY - 1 - i)
-        q = buf[g, 0].reshape(CH, D)
-        d = buf[g, 1].reshape(CH, D)
-        lse, delta = whole_stats(g)
-        f = jnp.exp2(mst[g] - lse)
-        acc = jnp.zeros((D, CH), F32)
-        for b in range(NB):
-            p = wbuf[g, b] * f
-            ds = (p * (dpbuf[g, b] - delta)).astype(BF)
-            rows = slice(b * TB, (b + 1) * TB)
-            dv[rows] = dv[rows] + dot_nn(p.astype(BF), d)
-            dk[rows] = dk[rows] + dot_nn(ds, q)
-            acc = acc + dot_nn(kt[:, rows], ds)
-        out = (acc * SCALE).astype(BF)
+        out = (dot_nn(kt[...], dsbuf[g].reshape(TOKENS, CH)) * SCALE).astype(BF)
 
         @pl.when(g == y)
         def _():
@@ -293,16 +329,7 @@
 
         return 0
 
-    lax.fori_loop(0, NY, backward, 0)
-
-    def rs_copy(src, dst):
-        return remote(rssend.at[dst], rsrecv.at[src], rs_send.at[dst], rs_recv.at[src], at_x(dst, c))
-
-    for t in range(NX):
-        rssend[t, 0] = (dk[t * QT:(t + 1) * QT] * SCALE).astype(BF)
-        rssend[t, 1] = dv[t * QT:(t + 1) * QT].astype(BF)
-    for j in (2, 1, 3):
-        rs_copy(x, lax.rem(x + j, NX)).start()
+    lax.fori_loop(0, NY, query_chunk, 0)
 
     def o_wait(j, _):
         t = lax.rem(y + j, NY)
@@ -315,28 +342,6 @@
     for t in range(NY):
         acc = acc + orecv[t].astype(F32) * jnp.exp2(stats[zh * NY + t, y, 0] - lse)
     fsend[0] = acc.T.astype(BF).reshape(COL, PIECE, D)
-
-    def q_wait(j, _):
-        t = lax.rem(y + j, NY)
-        remote(dqsend.at[t], dqrecv.at[t], q_send.at[t], q_recv.at[t], at_y(t)).wait_recv()
-        return 0
-
-    lax.fori_loop(1, NY, q_wait, 0)
-    acc = jnp.zeros((D, CH), F32)
-    for t in range(NY):
-        acc = acc + dqrecv[t].astype(F32)
-    fsend[1] = acc.T.astype(BF).reshape(COL, PIECE, D)
-
-    def f_copy(src, dst):
-        return remote(fsend.at[:, dst], frecv.at[src], f_send.at[dst], f_recv.at[src], column(dst))
-
-    def f_start(j, _):
-        f_copy(s, lax.rem(s + j, COL)).start()
-        return 0
-
-    lax.fori_loop(1, COL, f_start, 0)
-    frecv[s, 0] = fsend[0, s]
-    frecv[s, 1] = fsend[1, s]
 
     for j in range(1, NX):
         rs_copy(lax.rem(x + j, NX), x).wait_recv()
@@ -348,23 +353,53 @@
 
     core = lax.div(x, 2)
     part = lax.rem(x, 2)
-
-    def ag_copy(t):
+    grads = (kout, vout)
+
+    def spot(ref, pp, hh):
+        return ref.at[
+            pl.ds(pl.multiple_of(pp * QT, QT), QT), pl.ds(pl.multiple_of(hh * D, D), D)
+        ]
+
+    def ag_copy(a, t):
         return remote(
-            agsrc, kvout.at[:, part, c], ag_send.at[t], ag_recv.at[part, c], at_x(t, core)
+            agsrc.at[a], spot(grads[a], part, c), ag_send.at[a, t], ag_recv.at[a, part, c], at_x(t, core)
         )
 
     for j in (2, 1, 3):
-        ag_copy(lax.rem(x + j, NX)).start()
+        for a in range(2):
+            ag_copy(a, lax.rem(x + j, NX)).start()
 
     @pl.when(core != c)
     def _():
-        ag_copy(x).start()
+        ag_copy(0, x).start()
+        ag_copy(1, x).start()
 
     @pl.when(core == c)
     def _():
-        kvout[0, part, c] = agsrc[0]
-        kvout[1, part, c] = agsrc[1]
+        for a in range(2):
+            spot(grads[a], part, c)[...] = agsrc[a]
+
+    def q_wait(j, _):
+        t = lax.rem(y + j, NY)
+        remote(dqsend.at[t], dqrecv.at[t], q_send.at[t], q_recv.at[t], at_y(t)).wait_recv()
+        return 0
+
+    lax.fori_loop(1, NY, q_wait, 0)
+    acc = jnp.zeros((D, CH), F32)
+    for t in range(NY):
+        acc = acc + dqrecv[t].astype(F32)
+    fsend[1] = acc.T.astype(BF).reshape(COL, PIECE, D)
+
+    def f_copy(src, dst):
+        return remote(fsend.at[:, dst], frecv.at[src], f_send.at[dst], f_recv.at[src], column(dst))
+
+    def f_start(j, _):
+        f_copy(s, lax.rem(s + j, COL)).start()
+        return 0
+
+    lax.fori_loop(1, COL, f_start, 0)
+    frecv[s, 0] = fsend[0, s]
+    frecv[s, 1] = fsend[1, s]
 
     def f_wait(j, _):
         f_copy(lax.rem(s + j, COL), s).wait_recv()
@@ -372,8 +407,8 @@
 
     lax.fori_loop(1, COL, f_wait, 0)
     for h in range(KV):
-        for a in range(2):
-            fin[a, h] = (frecv[h, a].astype(F32) + frecv[KV + h, a].astype(F32)).astype(BF)
+        fin_o[h] = (frecv[h, 0].astype(F32) + frecv[KV + h, 0].astype(F32)).astype(BF)
+        fin_q[h] = (frecv[h, 1].astype(F32) + frecv[KV + h, 1].astype(F32)).astype(BF)
 
     for pp in range(2):
         for hh in range(2):
@@ -381,9 +416,11 @@
 
             @pl.when(jnp.logical_not(itself))
             def _():
-                remote(
-                    agsrc, kvout.at[:, pp, hh], ag_send.at[0], ag_recv.at[pp, hh], at_x(x, other)
-                ).wait_recv()
+                for a in range(2):
+                    remote(
+                        agsrc.at[a], spot(grads[a], pp, hh), ag_send.at[a, 0], ag_recv.at[a, pp, hh],
+                        at_x(x, other),
+                    ).wait_recv()
 
     def col_sent(j, _):
         t = lax.rem(s + j, COL)
@@ -416,11 +453,13 @@
     lax.fori_loop(1, CHIPS, s_sent, 0)
     for j in range(1, NX):
         rs_copy(x, lax.rem(x + j, NX)).wait_send()
-        ag_copy(lax.rem(x + j, NX)).wait_send()
+        for a in range(2):
+            ag_copy(a, lax.rem(x + j, NX)).wait_send()
 
     @pl.when(core != c)
     def _():
-        ag_copy(x).wait_send()
+        ag_copy(0, x).wait_send()
+        ag_copy(1, x).wait_send()
 
 
 def per_device(queries, output_gradient, keys, values, text_video, video_blocks):
@@ -437,15 +476,17 @@
     vm = pl.BlockSpec(memory_space=pltpu.VMEM)
     hbm = pl.BlockSpec(memory_space=pl.ANY)
     dma = pltpu.SemaphoreType.DMA
-    fin, kvout = pl.pallas_call(
+    fin_o, fin_q, key_grad, value_grad = pl.pallas_call(
         kernel,
         name="attention_step",
         out_shape=(
-            jax.ShapeDtypeStruct((2, KV, PIECE, D), BF),
-            jax.ShapeDtypeStruct((2, 2, 2, QT, D), BF),
+            jax.ShapeDtypeStruct((KV, PIECE, D), BF),
+            jax.ShapeDtypeStruct((KV, PIECE, D), BF),
+            jax.ShapeDtypeStruct((TOK, 2 * D), BF),
+            jax.ShapeDtypeStruct((TOK, 2 * D), BF),
         ),
         in_specs=[vm, hbm, hbm, vm],
-        out_specs=(vm, vm),
+        out_specs=(vm, vm, vm, vm),
         scratch_shapes=[
             pltpu.VMEM((NY, 2, COL, PIECE, D), BF),
             pltpu.VMEM((NC, TOK, D), BF),
@@ -454,14 +495,17 @@
             pltpu.VMEM((D, TOKENS), BF),
             pltpu.VMEM((NY, NB, TB, CH), F32),
             pltpu.VMEM((NY, NB, TB, CH), F32),
+            pltpu.VMEM((NY, NB, TB, CH), BF),
+            pltpu.VMEM((NY, 1, CH), F32),
+            pltpu.VMEM((NY, 1, CH), F32),
             pltpu.VMEM((NY, 1, CH), F32),
             pltpu.VMEM((CHIPS, NY, 2, 1, CH), F32),
             pltpu.VMEM((NY, D, CH), BF),
             pltpu.VMEM((NY, D, CH), BF),
             pltpu.VMEM((NY, D, CH), BF),
             pltpu.VMEM((NY, D, CH), BF),
-            pltpu.VMEM((TOKENS, D), F32),
-            pltpu.VMEM((TOKENS, D), F32),
+            pltpu.VMEM((QT, D), F32),
+            pltpu.VMEM((QT, D), F32),
             pltpu.VMEM((NX, 2, QT, D), BF),
             pltpu.VMEM((NX, 2, QT, D), BF),
             pltpu.VMEM((2, QT, D), BF),
@@ -474,15 +518,17 @@
             dma((CHIPS,)), dma((CHIPS,)),
             dma((NX,)), dma((NX,)),
             dma((COL,)), dma((COL,)),
-            dma((NX,)), dma((2, 2)),
+            dma((2, NX)), dma((2, 2, 2)),
         ],
         compiler_params=pltpu.CompilerParams(
             collective_id=0, has_side_effects=True, vmem_limit_bytes=56 * 1024 * 1024
         ),
     )(xin, keys, values, nvis)
-    out = fin.reshape(2, KV, ROWS, GROUP, D).transpose(0, 2, 1, 3, 4).reshape(2, ROWS, HEADS * D)
-    grads = kvout.transpose(0, 1, 3, 2, 4).reshape(2, TOK, 2 * D)
-    return out[0], out[1], grads[0], grads[1]
+
+    def flat(a):
+        return a.reshape(KV, ROWS, GROUP, D).transpose(1, 0, 2, 3).reshape(ROWS, HEADS * D)
+
+    return flat(fin_o), flat(fin_q), key_grad, value_grad
 
 
 def solution(mesh):

time: 92 us -> 86.6 us (0.941)
  Pallas kernels: 83.2 us -> 78 us
    pallas_call x1, Pallas kernels: 83.2 us -> 78 us  [per_device(): pl.pallas_call(kernel, name='attention_step', out_shape=(jax.ShapeDtypeSt...]
    unnamed x12 -> x18, local copies, waits for them, and re-layouts: 2.32 us -> 5.42 us
    slice x6 -> x0, local copies, waits for them, and re-layouts: 2 us -> none  [per_device(): return (out[0], out[1], grads[0], grads[1])]
    squeeze x2 -> x0, local copies, waits for them, and re-layouts: 1.26 us -> none  [per_device(): return (out[0], out[1], grads[0], grads[1])]
where the time goes in v2:
time: 86.6 us; the launch traced here: 86.3 us
  Pallas kernels  78 us (90%)
  local copies, waits for them, and re-layouts  6.87 us (8%)
    pallas_call x1, Pallas kernels, per_device(): pl.pallas_call(kernel, name='attention_step', out_shape=(jax.ShapeDtypeSt...  78 us
    unnamed x18, local copies, waits for them, and re-layouts  5.42 us

profile of v2, /device:TPU:1, one launch (start us, length us, event | category | flops | bytes accessed | tf_op | source)
XLA Modules:
  0.0 86.3 jit_solution(1127620022481461166)
XLA Ops:
  0.6 0.0 copy-start.4
  0.7 0.0 copy-start.5
  0.7 0.7 copy-done.4
  1.3 0.0 copy-done.5
  1.3 0.1 select_reduce_fusion
  1.4 0.1 min.12
  1.6 0.3 copy.23
  1.9 0.2 broadcast_in_dim.18
  2.1 0.0 copy-start.2
  2.1 0.0 copy-start.3
  2.1 0.8 reshape.41.nvis
  2.9 0.0 copy-done.2
  2.9 0.0 copy-done.3
  2.9 0.6 copy_bitcast_fusion.xin
  3.6 78.0 %attention_step.1 = (bf16[8,16,128]{2,1,0:T(8,128)(2,1)}, bf16[8,16,128]{2,1,0:T(8,128)(2,1)}, bf16[768,256]{1,0:T(8,128)(2,1)}, bf16[768,256]{1,0:T(8,128)(2,1)}) custom-call(bf16[8,2,16,128]{3,2,1,0:T(8,128)(2,1)} %copy_bitcast_fusion.xin, bf16[768,256]{1,0:T(8,128)(2,1)} %keys.1, bf16[768,256]{1,0:T(8,128)(2,1)} %values.1, s32[8,1,256]{2,1,0:T(1,128)} %reshape.41.nvis), custom_call_target="tpu_custom_call" | custom-call | tf_op jit(solution)/shard_map/attention_step/pallas_call | solution.py:479
  81.6 0.8 copy_bitcast_fusion.6
  82.3 0.0 copy-start.1
  82.3 0.6 copy.39
  83.0 0.1 copy-done.1
  83.1 0.6 copy.38
  83.7 0.0 copy-start
  83.7 1.8 %copy.42 = bf16[768,256]{1,0:T(8,128)(2,1)} copy(bf16[768,256]{1,0:T(8,128)(2,1)} %get-tuple-element.20) | data formatting | bytes 786432
  85.5 0.0 copy-done
  85.6 0.7 copy.43
  (3 shorter events, 0.0 us)
Async XLA Ops:
  0.6 0.7 copy-start.4
  0.7 0.7 copy-start.5
  2.1 0.8 copy-start.2
  2.1 0.8 copy-start.3
  82.3 0.8 copy-start.1
  83.7 1.8 %copy-start = (bf16[768,256]{1,0:T(8,128)(2,1)S(1)}, bf16[768,256]{1,0:T(8,128)(2,1)}, u32[]{:S(2)}) copy-start(bf16[768,256]{1,0:T(8,128)(2,1)} %get-tuple-element.21) | copy-start | bytes 1179652

commit v3 on v2

--- a/solution.py
+++ b/solution.py
@@ -22,6 +22,7 @@
 PIECE = ROWS * GROUP
 CH = COL * PIECE
 TOK = 768
+VIDEOS = 96
 TOKENS = NC * TOK
 TB = 384
 NB = TOKENS // TB
@@ -45,9 +46,9 @@
 
 
 def kernel(
-    xin, keys, values, nvis,
+    xin, keys, values, last_seen, video_blocks,
     fin_o, fin_q, kout, vout,
-    buf, kbuf, vbuf, kt, vt, wbuf, dpbuf, dsbuf, mst, fst, dst, stats,
+    nvis, buf, kbuf, vbuf, kt, vt, wbuf, dpbuf, dsbuf, pbuf, mst, stats,
     osend, orecv, dqsend, dqrecv, dk, dv, rssend, rsrecv, agsrc, fsend, frecv,
     a_send, a_recv, kv_send, kv_recv, kv_loc, r_send, r_recv, o_send, o_recv, q_send, q_recv,
     s_send, s_recv, rs_send, rs_recv, f_send, f_recv, ag_send, ag_recv,
@@ -104,6 +105,23 @@
             pl.semaphore_signal(
                 barrier, inc=1, device_id=at_x(lax.rem(x + j, NX), core), device_id_type=MESH
             )
+
+    seen_last = last_seen[...]
+    ends = jnp.zeros(seen_last.shape, jnp.int32)
+    for v in range(VIDEOS):
+        ends = ends + jnp.where(seen_last >= v, video_blocks[v], 0)
+    frames = TOKENS // FRAME
+    counts = jnp.clip(ends - n * frames, 0, frames).astype(F32).astype(BF)
+    lane = lax.broadcasted_iota(jnp.int32, (NZH * NY * NC * NK, CH), 1)
+    group = lax.broadcasted_iota(jnp.int32, (NZH * NY * NC * NK, CH), 0)
+    piece = lane // PIECE
+    wanted = ((piece // (NK * NC)) * NY * NC + piece % NC) * NK + (piece // NC) % NK
+    row = lax.broadcasted_iota(jnp.int32, (1, CH), 1) % ROWS
+    for g in range(NY):
+        pick = jnp.where(group == wanted + g * (NC * NK), 1.0, 0.0).astype(BF)
+        both = dot_nn(counts, pick)
+        nvis[g] = jnp.where(row == 0, both[0:1], both[1:2])
+
     pl.semaphore_wait(barrier, (COL - 1) + (CHIPS - 1) + 2 * (NX - 1))
 
     def a_copy(src_s, dst_s, dev):
@@ -137,19 +155,23 @@
     right = at_y(lax.rem(y + 1, NY))
     left = at_y(lax.rem(y + NY - 1, NY))
 
-    def ring(way, kind, t):
+    def ring_piece(way, kind, h, t, g):
+        ref = buf.at[g, kind, pl.ds(h * (COL // 2), COL // 2)]
+        return remote(
+            ref, ref, r_send.at[way, kind, h, t], r_recv.at[way, kind, h, t], right if way == 0 else left
+        )
+
+    def ring(way, kind, h, t):
         g = lax.rem(y + NY - t, NY) if way == 0 else lax.rem(y + t, NY)
-        ref = buf.at[g, kind]
-        return remote(ref, ref, r_send.at[way, kind, t], r_recv.at[way, kind, t], right if way == 0 else left)
-
-    def ring_arrival(way, kind, t):
+        return ring_piece(way, kind, h, t, g)
+
+    def ring_arrival(way, kind, h, t):
         g = lax.rem(y + NY - 1 - t, NY) if way == 0 else lax.rem(y + 1 + t, NY)
-        ref = buf.at[g, kind]
-        return remote(ref, ref, r_send.at[way, kind, t], r_recv.at[way, kind, t], right if way == 0 else left)
-
-    for kind in range(2):
-        for way in range(2):
-            ring(way, kind, 0).start()
+        return ring_piece(way, kind, h, t, g)
+
+    pieces = [(way, kind, h) for kind in range(2) for h in range(2) for way in range(2)]
+    for way, kind, h in pieces:
+        ring(way, kind, h, 0).start()
 
     kcopy.wait_recv()
     vcopy.wait_recv()
@@ -165,8 +187,8 @@
         h = b * TB // TOK
         return ref[h, b * TB - h * TOK:(b + 1) * TB - h * TOK]
 
-    def stats_out(i):
-        ref = stats.at[n, chunk_at(i)]
+    def stats_out(first, count):
+        ref = stats.at[n, pl.ds(first, count)]
 
         def s_start(j, _):
             t = lax.rem(n + j, CHIPS)
@@ -179,32 +201,25 @@
         @pl.when(lax.rem(i, 2) == 1)
         def _():
             t = lax.div(i - 1, 2)
-            for kind in range(2):
-                for way in range(2):
-                    last_too = kind == way
-
-                    if last_too:
-                        ring_arrival(way, kind, t).wait_recv()
-
-                        @pl.when(t < 3)
-                        def _():
-                            ring(way, kind, t + 1).start()
-                    else:
-                        @pl.when(t < 3)
-                        def _():
-                            ring_arrival(way, kind, t).wait_recv()
-
-                        @pl.when(t < 2)
-                        def _():
-                            ring(way, kind, t + 1).start()
+            for way, kind, h in pieces:
+                if kind == way:
+                    ring_arrival(way, kind, h, t).wait_recv()
+
+                    @pl.when(t < 3)
+                    def _():
+                        ring(way, kind, h, t + 1).start()
+                else:
+                    @pl.when(t < 3)
+                    def _():
+                        ring_arrival(way, kind, h, t).wait_recv()
+
+                    @pl.when(t < 2)
+                    def _():
+                        ring(way, kind, h, t + 1).start()
 
         @pl.when(i == 5)
         def _():
-            def early(e, _):
-                stats_out(e)
-                return 0
-
-            lax.fori_loop(0, 5, early, 0)
+            stats_out(0, 5)
 
         g = chunk_at(i)
         q = buf[g, 0].reshape(CH, D)
@@ -216,7 +231,7 @@
             wbuf[g, b] = sc
             for u in range(TB // FRAME):
                 part = jnp.max(sc[u * FRAME:(u + 1) * FRAME], axis=0, keepdims=True)
-                top = jnp.maximum(top, jnp.where(nv > b * (TB // FRAME) + u, part, NEG))
+                top = jnp.maximum(top, jnp.where(nv > float(b * (TB // FRAME) + u), part, NEG))
         msc = top * CS
         total = jnp.zeros((1, CH), F32)
         dsum = jnp.zeros((1, CH), F32)
@@ -226,29 +241,30 @@
             dpbuf[g, b] = dp
             ws = []
             for u in range(TB // FRAME):
-                bias = jnp.where(nv > b * (TB // FRAME) + u, -msc, NEG)
+                bias = jnp.where(nv > float(b * (TB // FRAME) + u), -msc, NEG)
                 ws.append(jnp.exp2(wbuf[g, b, u * FRAME:(u + 1) * FRAME] * CS + bias))
             w = jnp.concatenate(ws, axis=0)
             wbuf[g, b] = w
             total = total + jnp.sum(w, axis=0, keepdims=True)
             dsum = dsum + jnp.sum(w * dp, axis=0, keepdims=True)
             acc = acc + dot_nn(vt[:, b * TB:(b + 1) * TB], w.astype(BF))
-        seen = nv > 0
+        seen = nv > 0.0
         inv = jnp.where(seen, 1.0 / jnp.where(seen, total, 1.0), 0.0)
-        stats[n, g, 0] = jnp.where(seen, msc + jnp.log2(jnp.where(seen, total, 1.0)), NEG)
-        stats[n, g, 1] = dsum * inv
+        stats[n, i, 0] = jnp.where(seen, msc + jnp.log2(jnp.where(seen, total, 1.0)), NEG)
+        stats[n, i, 1] = dsum * inv
         mst[g] = msc
         out = (acc * inv).astype(BF)
 
         osend[g] = out
 
-        @pl.when(i >= 5)
+        @pl.when(i == 6)
         def _():
-            stats_out(i)
+            stats_out(5, 2)
 
         return 0
 
     lax.fori_loop(0, NY, forward, 0)
+    stats_out(NY - 1, 1)
 
     def o_start(j, _):
         g = chunk_at(NY - 1 - j)
@@ -266,57 +282,34 @@
 
     lax.fori_loop(1, CHIPS, s_wait, 0)
 
+    def order_at(t, g):
+        r = lax.rem(g + NY - t % NY, NY)
+        return jnp.where(r < 4, 2 * r, jnp.where(r == 4, NY - 1, 2 * NY - 1 - 2 * r))
+
     def whole_stats(g):
-        peak = stats[0, g, 0]
-        for t in range(1, CHIPS):
-            peak = jnp.maximum(peak, stats[t, g, 0])
+        at = [order_at(t, g) for t in range(NY)]
+        tops = [stats[t, at[t % NY], 0] for t in range(CHIPS)]
+        peak = functools.reduce(jnp.maximum, tops)
         mass = jnp.zeros((1, CH), F32)
         dsum = jnp.zeros((1, CH), F32)
         for t in range(CHIPS):
-            e = jnp.exp2(stats[t, g, 0] - peak)
+            e = jnp.exp2(tops[t] - peak)
             mass = mass + e
-            dsum = dsum + e * stats[t, g, 1]
+            dsum = dsum + e * stats[t, at[t % NY], 1]
         return peak + jnp.log2(mass), dsum / mass
-
-    def prepare(g, _):
-        lse, delta = whole_stats(g)
-        fst[g] = jnp.exp2(mst[g] - lse)
-        dst[g] = delta
-        return 0
-
-    lax.fori_loop(0, NY, prepare, 0)
-
-    def rs_copy(src, to):
-        return remote(rssend.at[to], rsrecv.at[src], rs_send.at[to], rs_recv.at[src], at_x(to, c))
-
-    for j in (2, 1, 3, 0):
-        b = lax.rem(x + j, NX)
-        dk[...] = jnp.zeros_like(dk)
-        dv[...] = jnp.zeros_like(dv)
-
-        def quarter(g, _):
-            q = buf[g, 0].reshape(CH, D)
-            d = buf[g, 1].reshape(CH, D)
-            f = fst[g]
-            delta = dst[g]
-            for u in range(QT // FRAME):
-                rows = slice(u * FRAME, (u + 1) * FRAME)
-                p = wbuf[g, b, rows] * f
-                ds = (p * (dpbuf[g, b, rows] - delta)).astype(BF)
-                dsbuf[g, b, rows] = ds
-                dv[rows] = dv[rows] + dot_nn(p.astype(BF), d)
-                dk[rows] = dk[rows] + dot_nn(ds, q)
-            return 0
-
-        lax.fori_loop(0, NY, quarter, 0)
-        rssend[b, 0] = (dk[...] * SCALE).astype(BF)
-        rssend[b, 1] = dv[...].astype(BF)
-        if j:
-            rs_copy(x, b).start()
 
     def query_chunk(i, _):
         g = chunk_at(NY - 1 - i)
-        out = (dot_nn(kt[...], dsbuf[g].reshape(TOKENS, CH)) * SCALE).astype(BF)
+        lse, delta = whole_stats(g)
+        f = jnp.exp2(mst[g] - lse)
+        acc = jnp.zeros((D, CH), F32)
+        for b in range(NB):
+            p = wbuf[g, b] * f
+            ds = (p * (dpbuf[g, b] - delta)).astype(BF)
+            pbuf[g, b] = p.astype(BF)
+            dsbuf[g, b] = ds
+            acc = acc + dot_nn(kt[:, b * TB:(b + 1) * TB], ds)
+        out = (acc * SCALE).astype(BF)
 
         @pl.when(g == y)
         def _():
@@ -331,6 +324,33 @@
 
     lax.fori_loop(0, NY, query_chunk, 0)
 
+    def rs_copy(src, to):
+        return remote(rssend.at[to], rsrecv.at[src], rs_send.at[to], rs_recv.at[src], at_x(to, c))
+
+    def quarter(j, _):
+        away = jnp.where(j == 0, 2, jnp.where(j == 1, 1, jnp.where(j == 2, 3, 0)))
+        b = lax.rem(x + away, NX)
+        for g in range(NY):
+            part_v = dot_nn(pbuf[g, b], buf[g, 1].reshape(CH, D))
+            part_k = dot_nn(dsbuf[g, b], buf[g, 0].reshape(CH, D))
+            if g == 0:
+                dv[...] = part_v
+                dk[...] = part_k
+            elif g < NY - 1:
+                dv[...] = dv[...] + part_v
+                dk[...] = dk[...] + part_k
+            else:
+                rssend[b, 1] = (dv[...] + part_v).astype(BF)
+                rssend[b, 0] = ((dk[...] + part_k) * SCALE).astype(BF)
+
+        @pl.when(j < NX - 1)
+        def _():
+            rs_copy(x, b).start()
+
+        return 0
+
+    lax.fori_loop(0, NX, quarter, 0)
+
     def o_wait(j, _):
         t = lax.rem(y + j, NY)
         remote(osend.at[t], orecv.at[t], o_send.at[t], o_recv.at[t], at_y(t)).wait_recv()
@@ -340,8 +360,21 @@
     lse, _ = whole_stats(y)
     acc = jnp.zeros((D, CH), F32)
     for t in range(NY):
-        acc = acc + orecv[t].astype(F32) * jnp.exp2(stats[zh * NY + t, y, 0] - lse)
+        acc = acc + orecv[t].astype(F32) * jnp.exp2(stats[zh * NY + t, order_at(t, y), 0] - lse)
     fsend[0] = acc.T.astype(BF).reshape(COL, PIECE, D)
+
+    def f_copy(a, src, to):
+        return remote(fsend.at[a, to], frecv.at[a, src], f_send.at[a, to], f_recv.at[a, src], column(to))
+
+    def f_push(a):
+        def start(j, _):
+            f_copy(a, s, lax.rem(s + j, COL)).start()
+            return 0
+
+        lax.fori_loop(1, COL, start, 0)
+        frecv[a, s] = fsend[a, s]
+
+    f_push(0)
 
     for j in range(1, NX):
         rs_copy(lax.rem(x + j, NX), x).wait_recv()
@@ -390,25 +423,17 @@
         acc = acc + dqrecv[t].astype(F32)
     fsend[1] = acc.T.astype(BF).reshape(COL, PIECE, D)
 
-    def f_copy(src, dst):
-        return remote(fsend.at[:, dst], frecv.at[src], f_send.at[dst], f_recv.at[src], column(dst))
-
-    def f_start(j, _):
-        f_copy(s, lax.rem(s + j, COL)).start()
-        return 0
-
-    lax.fori_loop(1, COL, f_start, 0)
-    frecv[s, 0] = fsend[0, s]
-    frecv[s, 1] = fsend[1, s]
+    f_push(1)
 
     def f_wait(j, _):
-        f_copy(lax.rem(s + j, COL), s).wait_recv()
+        f_copy(0, lax.rem(s + j, COL), s).wait_recv()
+        f_copy(1, lax.rem(s + j, COL), s).wait_recv()
         return 0
 
     lax.fori_loop(1, COL, f_wait, 0)
     for h in range(KV):
-        fin_o[h] = (frecv[h, 0].astype(F32) + frecv[KV + h, 0].astype(F32)).astype(BF)
-        fin_q[h] = (frecv[h, 1].astype(F32) + frecv[KV + h, 1].astype(F32)).astype(BF)
+        fin_o[h] = (frecv[0, h].astype(F32) + frecv[0, KV + h].astype(F32)).astype(BF)
+        fin_q[h] = (frecv[1, h].astype(F32) + frecv[1, KV + h].astype(F32)).astype(BF)
 
     for pp in range(2):
         for hh in range(2):
@@ -425,16 +450,16 @@
     def col_sent(j, _):
         t = lax.rem(s + j, COL)
         a_copy(s, t, column(t)).wait_send()
-        f_copy(s, t).wait_send()
+        f_copy(0, s, t).wait_send()
+        f_copy(1, s, t).wait_send()
         return 0
 
     lax.fori_loop(1, COL, col_sent, 0)
     kcopy.wait_send()
     vcopy.wait_send()
-    for kind in range(2):
-        for way in range(2):
-            for t in range(4 if kind == way else 3):
-                ring(way, kind, t).wait_send()
+    for way, kind, h in pieces:
+        for t in range(4 if kind == way else 3):
+            ring(way, kind, h, t).wait_send()
 
     def y_sent(j, _):
         t = lax.rem(y + j, NY)
@@ -463,18 +488,11 @@
 
 
 def per_device(queries, output_gradient, keys, values, text_video, video_blocks):
-    n = lax.axis_index("mem") // 2
     both = jnp.stack([queries, output_gradient])
-    xin = both.reshape(2, ROWS, KV, GROUP, D).transpose(2, 0, 1, 3, 4).reshape(KV, 2, PIECE, D)
-    ids = jnp.arange(video_blocks.shape[0], dtype=jnp.int32)
-    ends = jnp.sum(jnp.where(ids <= text_video[..., None], video_blocks, 0), axis=-1)
-    frames = TOKENS // FRAME
-    seen = jnp.clip(ends - n * frames, 0, frames)
-    seen = seen.reshape(NZH, NY, NC, NK, ROWS).transpose(1, 0, 3, 2, 4)
-    nvis = jnp.broadcast_to(seen[..., None], (NY, NZH, NK, NC, ROWS, GROUP)).reshape(NY, 1, CH)
-
+    xin = both.reshape(2, ROWS, KV, GROUP, D).transpose(2, 0, 3, 1, 4).reshape(KV, 2, PIECE, D)
     vm = pl.BlockSpec(memory_space=pltpu.VMEM)
-    hbm = pl.BlockSpec(memory_space=pl.ANY)
+    hbm = pl.BlockSpec(memory_space=pltpu.HBM)
+    smem = pl.BlockSpec(memory_space=pltpu.SMEM)
     dma = pltpu.SemaphoreType.DMA
     fin_o, fin_q, key_grad, value_grad = pl.pallas_call(
         kernel,
@@ -485,9 +503,10 @@
             jax.ShapeDtypeStruct((TOK, 2 * D), BF),
             jax.ShapeDtypeStruct((TOK, 2 * D), BF),
         ),
-        in_specs=[vm, hbm, hbm, vm],
+        in_specs=[vm, hbm, hbm, vm, smem],
         out_specs=(vm, vm, vm, vm),
         scratch_shapes=[
+            pltpu.VMEM((NY, 1, CH), F32),
             pltpu.VMEM((NY, 2, COL, PIECE, D), BF),
             pltpu.VMEM((NC, TOK, D), BF),
             pltpu.VMEM((NC, TOK, D), BF),
@@ -496,8 +515,7 @@
             pltpu.VMEM((NY, NB, TB, CH), F32),
             pltpu.VMEM((NY, NB, TB, CH), F32),
             pltpu.VMEM((NY, NB, TB, CH), BF),
-            pltpu.VMEM((NY, 1, CH), F32),
-            pltpu.VMEM((NY, 1, CH), F32),
+            pltpu.VMEM((NY, NB, TB, CH), BF),
             pltpu.VMEM((NY, 1, CH), F32),
             pltpu.VMEM((CHIPS, NY, 2, 1, CH), F32),
             pltpu.VMEM((NY, D, CH), BF),
@@ -510,23 +528,29 @@
             pltpu.VMEM((NX, 2, QT, D), BF),
             pltpu.VMEM((2, QT, D), BF),
             pltpu.VMEM((2, COL, PIECE, D), BF),
-            pltpu.VMEM((COL, 2, PIECE, D), BF),
+            pltpu.VMEM((2, COL, PIECE, D), BF),
             dma((COL,)), dma((COL,)),
             dma((2,)), dma((2,)), dma((2,)),
-            dma((2, 2, 4)), dma((2, 2, 4)),
+            dma((2, 2, 2, 4)), dma((2, 2, 2, 4)),
             dma((NY,)), dma((NY,)), dma((NY,)), dma((NY,)),
             dma((CHIPS,)), dma((CHIPS,)),
             dma((NX,)), dma((NX,)),
-            dma((COL,)), dma((COL,)),
+            dma((2, COL)), dma((2, COL)),
             dma((2, NX)), dma((2, 2, 2)),
         ],
         compiler_params=pltpu.CompilerParams(
-            collective_id=0, has_side_effects=True, vmem_limit_bytes=56 * 1024 * 1024
+            collective_id=0, has_side_effects=True, vmem_limit_bytes=46 * 1024 * 1024
         ),
-    )(xin, keys, values, nvis)
+    )(
+        xin,
+        pltpu.with_memory_space_constraint(keys, pltpu.HBM),
+        pltpu.with_memory_space_constraint(values, pltpu.HBM),
+        text_video.T,
+        video_blocks,
+    )
 
     def flat(a):
-        return a.reshape(KV, ROWS, GROUP, D).transpose(1, 0, 2, 3).reshape(ROWS, HEADS * D)
+        return a.reshape(KV, GROUP, ROWS, D).transpose(2, 0, 1, 3).reshape(ROWS, HEADS * D)
 
     return flat(fin_o), flat(fin_q), key_grad, value_grad
 

time: 86.6 us -> 82.5 us (0.953)
  local copies, waits for them, and re-layouts: 6.87 us -> 3.39 us
    unnamed x18 -> x8, local copies, waits for them, and re-layouts: 5.42 us -> 3.39 us
    another operation x0 -> x1, other arithmetic: none -> 0.87 us  [per_device(): both = jnp.stack([queries, output_gradient])]
where the time goes in v3:
time: 82.5 us; the launch traced here: 82.3 us
  Pallas kernels  77.3 us (94%)
  local copies, waits for them, and re-layouts  3.39 us (4%)
  other arithmetic  0.87 us (1%)
    pallas_call x1, Pallas kernels, per_device(): pl.pallas_call(kernel, name='attention_step', out_shape=(jax.ShapeDtypeSt...  77.3 us
    unnamed x8, local copies, waits for them, and re-layouts  3.39 us

profile of v3, /device:TPU:1, one launch (start us, length us, event | category | flops | bytes accessed | tf_op | source)
XLA Modules:
  0.0 82.3 jit_solution(10312321222455722516)
XLA Ops:
  0.6 0.9 %pad_maximum_fusion = bf16[2,2,8,8,128]{4,1,3,0,2:T(2,128)(2,1)S(1)} fusion(bf16[1,2,8,8,128]{4,1,3,0,2:T(2,128)(2,1)} %bitcast.20, bf16[1,2,8,8,128]{4,1,3,0,2:T(2,128)(2,1)} %bitcast.21), kind=kLoop, calls=%fused_computation | loop fusion | flops 32768 | bytes 131072 | tf_op jit(solution)/shard_map/stack | solution.py:491
  1.5 0.0 copy-start
  1.5 0.0 copy-start.1
  1.5 0.7 copy-done
  2.2 0.0 copy-done.1
  2.2 77.3 %attention_step.1 = (bf16[8,16,128]{2,1,0:T(8,128)(2,1)S(1)}, bf16[8,16,128]{2,1,0:T(8,128)(2,1)S(1)}, bf16[768,256]{1,0:T(8,128)(2,1)S(1)}, bf16[768,256]{1,0:T(8,128)(2,1)S(1)}) custom-call(bf16[8,2,16,128]{3,2,1,0:T(8,128)(2,1)S(1)} %bitcast.16, bf16[768,256]{1,0:T(8,128)(2,1)} %keys.1, bf16[768,256]{1,0:T(8,128)(2,1)} %values.1, s32[2,128]{1,0:T(2,128)S(1)} %bitcast.19, ...), custom_call_target="tpu_custom_call" | custom-call | tf_op jit(solution)/shard_map/attention_step/pallas_call | solution.py:497
  79.5 0.6 copy.18
  80.2 0.6 copy.19
  80.8 0.7 copy.20
  81.5 0.7 copy.21
Async XLA Ops:
  1.5 0.7 copy-start
  1.5 0.7 copy-start.1

commit v4 on v3

--- a/solution.py
+++ b/solution.py
@@ -46,9 +46,9 @@
 
 
 def kernel(
-    xin, keys, values, last_seen, video_blocks,
+    queries, gradients, keys, values, last_seen_hbm, video_blocks_hbm,
     fin_o, fin_q, kout, vout,
-    nvis, buf, kbuf, vbuf, kt, vt, wbuf, dpbuf, dsbuf, pbuf, mst, stats,
+    xin, last_seen, video_blocks, in_loc, nvis, buf, kbuf, vbuf, kt, vt, wbuf, dpbuf, dsbuf, pbuf, mst, stats,
     osend, orecv, dqsend, dqrecv, dk, dv, rssend, rsrecv, agsrc, fsend, frecv,
     a_send, a_recv, kv_send, kv_recv, kv_loc, r_send, r_recv, o_send, o_recv, q_send, q_recv,
     s_send, s_recv, rs_send, rs_recv, f_send, f_recv, ag_send, ag_recv,
@@ -85,6 +85,14 @@
     other_cols = pl.ds(pl.multiple_of(other * D, D), D)
     loc_k = pltpu.make_async_copy(keys.at[:, mine_cols], kbuf.at[c], kv_loc.at[0])
     loc_v = pltpu.make_async_copy(values.at[:, mine_cols], vbuf.at[c], kv_loc.at[1])
+    into = [
+        pltpu.make_async_copy(queries, xin.at[:, 0], in_loc.at[0]),
+        pltpu.make_async_copy(gradients, xin.at[:, 1], in_loc.at[1]),
+        pltpu.make_async_copy(last_seen_hbm, last_seen, in_loc.at[2]),
+        pltpu.make_async_copy(video_blocks_hbm, video_blocks, in_loc.at[3]),
+    ]
+    for copy in into:
+        copy.start()
     loc_k.start()
     loc_v.start()
 
@@ -106,6 +114,8 @@
                 barrier, inc=1, device_id=at_x(lax.rem(x + j, NX), core), device_id_type=MESH
             )
 
+    for copy in into:
+        copy.wait()
     seen_last = last_seen[...]
     ends = jnp.zeros(seen_last.shape, jnp.int32)
     for v in range(VIDEOS):
@@ -488,11 +498,12 @@
 
 
 def per_device(queries, output_gradient, keys, values, text_video, video_blocks):
-    both = jnp.stack([queries, output_gradient])
-    xin = both.reshape(2, ROWS, KV, GROUP, D).transpose(2, 0, 3, 1, 4).reshape(KV, 2, PIECE, D)
+    def pieces(a):
+        a = a.reshape(ROWS, KV, GROUP, D).transpose(1, 2, 0, 3).reshape(KV, PIECE, D)
+        return pltpu.with_memory_space_constraint(a, pltpu.HBM)
+
     vm = pl.BlockSpec(memory_space=pltpu.VMEM)
     hbm = pl.BlockSpec(memory_space=pltpu.HBM)
-    smem = pl.BlockSpec(memory_space=pltpu.SMEM)
     dma = pltpu.SemaphoreType.DMA
     fin_o, fin_q, key_grad, value_grad = pl.pallas_call(
         kernel,
@@ -503,9 +514,13 @@
             jax.ShapeDtypeStruct((TOK, 2 * D), BF),
             jax.ShapeDtypeStruct((TOK, 2 * D), BF),
         ),
-        in_specs=[vm, hbm, hbm, vm, smem],
+        in_specs=[hbm] * 6,
         out_specs=(vm, vm, vm, vm),
         scratch_shapes=[
+            pltpu.VMEM((KV, 2, PIECE, D), BF),
+            pltpu.VMEM((ROWS, NZH * NY * NC * NK), jnp.int32),
+            pltpu.SMEM((VIDEOS,), jnp.int32),
+            dma((4,)),
             pltpu.VMEM((NY, 1, CH), F32),
             pltpu.VMEM((NY, 2, COL, PIECE, D), BF),
             pltpu.VMEM((NC, TOK, D), BF),
@@ -542,11 +557,12 @@
             collective_id=0, has_side_effects=True, vmem_limit_bytes=46 * 1024 * 1024
         ),
     )(
-        xin,
+        pieces(queries),
+        pieces(output_gradient),
         pltpu.with_memory_space_constraint(keys, pltpu.HBM),
         pltpu.with_memory_space_constraint(values, pltpu.HBM),
-        text_video.T,
-        video_blocks,
+        pltpu.with_memory_space_constraint(text_video.T, pltpu.HBM),
+        pltpu.with_memory_space_constraint(video_blocks, pltpu.HBM),
     )
 
     def flat(a):

time: 82.5 us -> 80.3 us (0.973)
  other arithmetic: 0.87 us -> 0 us
    another operation x1 -> x0, other arithmetic: 0.87 us -> none  [per_device(): both = jnp.stack([queries, output_gradient])]
    unnamed x8 -> x4, local copies, waits for them, and re-layouts: 3.39 us -> 2.72 us
where the time goes in v4:
time: 80.3 us; the launch traced here: 80.2 us
  Pallas kernels  76.8 us (96%)
  local copies, waits for them, and re-layouts  2.72 us (3%)
    pallas_call x1, Pallas kernels, per_device(): pl.pallas_call(kernel, name='attention_step', out_shape=(jax.ShapeDtypeSt...  76.8 us
    unnamed x4, local copies, waits for them, and re-layouts  2.72 us

profile of v4, /device:TPU:1, one launch (start us, length us, event | category | flops | bytes accessed | tf_op | source)
XLA Modules:
  0.0 80.2 jit_solution(10470500025901857905)
XLA Ops:
  0.6 76.8 %attention_step.1 = (bf16[8,16,128]{2,1,0:T(8,128)(2,1)S(1)}, bf16[8,16,128]{2,1,0:T(8,128)(2,1)S(1)}, bf16[768,256]{1,0:T(8,128)(2,1)S(1)}, bf16[768,256]{1,0:T(8,128)(2,1)S(1)}) custom-call(bf16[8,16,128]{2,1,0:T(8,128)(2,1)} %bitcast.23, bf16[8,16,128]{2,1,0:T(8,128)(2,1)} %bitcast.24, bf16[768,256]{1,0:T(8,128)(2,1)} %keys.1, bf16[768,256]{1,0:T(8,128)(2,1)} %values.1, ...), custom_call_target="tpu_custom_call" | custom-call | tf_op jit(solution)/shard_map/attention_step/pallas_call | solution.py:508
  77.5 0.6 copy.18
  78.1 0.6 copy.19
  78.7 0.7 copy.20
  79.5 0.7 copy.21
